TPU v7x, 64 devices: a 2x2x8 block of a 4x4x8 slice. The times are simulated.
64 devices in a mesh: graphs: 4 (over x, y), nodes: 16 (over z, core).
Axes of the slice: x: 2, y: 2, z: 8, core: 2. Of those that a mesh axis runs over, the one named last changes fastest.
The devices are a block of a 4x4x8 slice.
Arguments:
- x_feat: bfloat16 [32768, 512], P(('graphs', 'nodes')), parts along dimension 0
- valid: int32 [32768], P(('graphs', 'nodes')), parts along dimension 0
- halo_slot: int32 [64, 16, 32], P(('graphs', 'nodes')), parts along dimension 0
- edge_src: int32 [64, 25600], P(('graphs', 'nodes')), parts along dimension 0
- edge_dst: int32 [64, 25600], P(('graphs', 'nodes')), parts along dimension 0
- edge_mask: int32 [64, 25600], P(('graphs', 'nodes')), parts along dimension 0
- bal_perm: int32 [32768], P(('graphs', 'nodes')), parts along dimension 0
- pos_enc: bfloat16 [32768, 512], P(('graphs', 'nodes')), parts along dimension 0
- y_cot: bfloat16 [32768, 512], P(('graphs', 'nodes')), parts along dimension 0
- w_msg: bfloat16 [512, 512], replicated
- w_self: bfloat16 [512, 512], replicated
- w_q: bfloat16 [512, 512], replicated
- w_k: bfloat16 [512, 64], replicated
- w_v: bfloat16 [512, 64], replicated
- w_o: bfloat16 [512, 512], replicated
- w_up: bfloat16 [512, 2048], replicated
- w_down: bfloat16 [2048, 512], replicated
Outputs:
- output 1: bfloat16 [32768, 512], P(('graphs', 'nodes')), parts along dimension 0
- output 2: bfloat16 [32768, 512], P(('graphs', 'nodes')), parts along dimension 0
- output 3: float32 [2048, 512], P('graphs'), parts along dimension 0
- output 4: float32 [2048, 512], P('graphs'), parts along dimension 0
- output 5: float32 [2048, 512], P('graphs'), parts along dimension 0
- output 6: float32 [2048, 64], P('graphs'), parts along dimension 0
- output 7: float32 [2048, 64], P('graphs'), parts along dimension 0
- output 8: float32 [2048, 512], P('graphs'), parts along dimension 0
- output 9: float32 [2048, 2048], P('graphs'), parts along dimension 0
- output 10: float32 [8192, 512], P('graphs'), parts along dimension 0
There are 4 independent parts. A program takes and returns all parts, laid end to end along the dimension named above; an argument that names none is the same for every part.
All inputs are finite; a program needn't handle non-finite values.
Results may differ from a plain program's by a relative error of at most 0.02.
Values are sent between devices in bfloat16 or wider.
A program may use at most 768 MiB of HBM per device.

v0:
```python
import jax
import jax.numpy as jnp
from jax import lax
from jax.sharding import PartitionSpec as P

NEG_FILL = -1e30


def serve(source, wanted):
    picked = jnp.take(source, wanted.reshape(-1), axis=0, mode='clip')
    return lax.all_to_all(picked.reshape(wanted.shape + source.shape[1:]), 'nodes', 0, 0, tiled=True)


def deliver(rows, wanted, num_rows):
    landed = lax.all_to_all(rows, 'nodes', 0, 0, tiled=True)
    flat = landed.reshape((-1,) + landed.shape[2:]).astype(jnp.float32)
    return jax.ops.segment_sum(flat, wanted.reshape(-1), num_segments=num_rows + 1)[:num_rows]


def build_adjacency(edge_src, edge_dst, edge_mask, rows_dev, table_rows):
    counts = jnp.zeros((rows_dev, table_rows), jnp.float32).at[edge_dst, edge_src].add(edge_mask.astype(jnp.float32))
    return counts.astype(jnp.bfloat16)


def balanced_routes(bal_perm, rows_dev, nodes, capacity):
    owner_ix = bal_perm // rows_dev
    slot_ix = bal_perm % rows_dev
    one_hot = (owner_ix[:, None] == jnp.arange(nodes, dtype=jnp.int32)[None, :]).astype(jnp.int32)
    rank_ix = jnp.sum(jnp.cumsum(one_hot, axis=0) * one_hot, axis=1) - 1
    route_ix = owner_ix * capacity + rank_ix
    requests = jnp.full((nodes * capacity,), rows_dev, jnp.int32).at[route_ix].set(slot_ix).reshape(nodes, capacity)
    sources = jnp.zeros((nodes * capacity,), jnp.int32).at[route_ix].set(jnp.arange(rows_dev, dtype=jnp.int32))
    return route_ix, requests, sources


def attention_forward(q_rows, key_all, val_all, ok_all, scale):
    def shard_step(carry, shard):
        run_max, run_sum, weighted = carry
        key_blk, val_blk, ok_blk = shard
        scores = jnp.einsum('qe,ke->qk', q_rows, key_blk, preferred_element_type=jnp.float32) * scale
        scores = jnp.where(ok_blk[None, :] > 0, scores, NEG_FILL)
        new_max = jnp.maximum(run_max, jnp.max(scores, axis=1))
        prob_blk = jnp.exp(scores - new_max[:, None])
        decay = jnp.exp(run_max - new_max)
        run_sum = run_sum * decay + jnp.sum(prob_blk, axis=1)
        weighted = weighted * decay[:, None] + jnp.dot(prob_blk.astype(jnp.bfloat16), val_blk, preferred_element_type=jnp.float32)
        return (new_max, run_sum, weighted), None

    num_rows = q_rows.shape[0]
    start_state = (jnp.full((num_rows,), -jnp.inf, jnp.float32), jnp.zeros((num_rows,), jnp.float32), jnp.zeros((num_rows, val_all.shape[-1]), jnp.float32))
    final_state, unused = lax.scan(shard_step, start_state, (key_all, val_all, ok_all))
    run_max, run_sum, weighted = final_state
    return weighted / run_sum[:, None], run_max + jnp.log(run_sum)


def attention_backward(q_rows, key_all, val_all, ok_all, scale, log_norm, d_mixed, delta):
    def shard_step(dq_sum, shard):
        key_blk, val_blk, ok_blk = shard
        scores = jnp.einsum('qe,ke->qk', q_rows, key_blk, preferred_element_type=jnp.float32) * scale
        scores = jnp.where(ok_blk[None, :] > 0, scores, NEG_FILL)
        prob_blk = jnp.exp(scores - log_norm[:, None])
        dv_blk = jnp.einsum('qk,qe->ke', prob_blk.astype(jnp.bfloat16), d_mixed, preferred_element_type=jnp.float32)
        d_prob = jnp.einsum('qe,ke->qk', d_mixed, val_blk, preferred_element_type=jnp.float32)
        d_scores = (prob_blk * (d_prob - delta[:, None])).astype(jnp.bfloat16)
        dq_sum = dq_sum + jnp.dot(d_scores, key_blk, preferred_element_type=jnp.float32)
        dk_blk = jnp.einsum('qk,qe->ke', d_scores, q_rows, preferred_element_type=jnp.float32)
        return dq_sum, (dk_blk, dv_blk)

    dq_sum, shard_grads = lax.scan(shard_step, jnp.zeros(q_rows.shape, jnp.float32), (key_all, val_all, ok_all))
    dk_all, dv_all = shard_grads
    return dq_sum * scale, dk_all * scale, dv_all


def solution(mesh):
    nodes = mesh.shape['nodes']
    row_spec = P(('graphs', 'nodes'), None)
    flat_spec = P(('graphs', 'nodes'))
    halo_spec = P(('graphs', 'nodes'), None, None)
    grad_spec = P('graphs', None)

    def device_step(x_feat, valid, halo_slot, edge_src, edge_dst, edge_mask, bal_perm, pos_enc, y_cot, w_msg, w_self, w_q, w_k, w_v, w_o, w_up, w_down):
        rows_dev, width = x_feat.shape
        head_dim = w_k.shape[1]
        heads = width // head_dim
        scale = head_dim ** -0.5
        capacity = rows_dev // nodes + rows_dev // (2 * nodes)
        halo_req = halo_slot.reshape(nodes, -1)
        halo_rows = halo_req.size
        halo_got = lax.all_to_all(halo_req, 'nodes', 0, 0, tiled=True)
        halo_feat = serve(x_feat, halo_got).reshape(halo_rows, width)
        adjacency = build_adjacency(edge_src.reshape(-1), edge_dst.reshape(-1), edge_mask.reshape(-1), rows_dev, rows_dev + halo_rows)
        table = jnp.concatenate([x_feat, halo_feat], axis=0)
        agg_msg = jnp.dot(adjacency, table, preferred_element_type=jnp.float32).astype(jnp.bfloat16)
        pre_act = jnp.dot(agg_msg, w_msg, preferred_element_type=jnp.float32) + jnp.dot(x_feat, w_self, preferred_element_type=jnp.float32)

        route_ix, requests, sources = balanced_routes(bal_perm, rows_dev, nodes, capacity)
        wanted = lax.all_to_all(requests, 'nodes', 0, 0, tiled=True)
        x_bal = serve(x_feat, wanted).reshape(nodes * capacity, width)[route_ix]
        ok_bal = serve(valid, wanted).reshape(nodes * capacity)[route_ix]
        hidden_in = (x_bal.astype(jnp.float32) + pos_enc.astype(jnp.float32)).astype(jnp.bfloat16)
        q_rows = jnp.dot(hidden_in, w_q, preferred_element_type=jnp.float32).astype(jnp.bfloat16).reshape(rows_dev * heads, head_dim)
        key_loc = jnp.dot(hidden_in, w_k, preferred_element_type=jnp.float32).astype(jnp.bfloat16)
        val_loc = jnp.dot(hidden_in, w_v, preferred_element_type=jnp.float32).astype(jnp.bfloat16)
        key_all = lax.all_gather(key_loc, 'nodes')
        val_all = lax.all_gather(val_loc, 'nodes')
        ok_all = lax.all_gather(ok_bal, 'nodes')
        mixed_wide, log_norm = attention_forward(q_rows, key_all, val_all, ok_all, scale)
        mixed = mixed_wide.astype(jnp.bfloat16)
        mixed_rows = mixed.reshape(rows_dev, width)
        u_bal = jnp.dot(mixed_rows, w_o, preferred_element_type=jnp.float32).astype(jnp.bfloat16)
        u_part = deliver(jnp.take(u_bal, sources, axis=0).reshape(nodes, capacity, width), wanted, rows_dev)
        x_wide = x_feat.astype(jnp.float32)
        z_mid = (x_wide + jax.nn.relu(pre_act) + x_wide + u_part).astype(jnp.bfloat16)
        h_pre = jnp.dot(z_mid, w_up, preferred_element_type=jnp.float32)
        hidden = jax.nn.gelu(h_pre).astype(jnp.bfloat16)
        keep_row = valid[:, None] > 0
        y_out = jnp.where(keep_row, z_mid.astype(jnp.float32) + jnp.dot(hidden, w_down, preferred_element_type=jnp.float32), 0.0).astype(jnp.bfloat16)

        g_out = jnp.where(keep_row, y_cot, jnp.zeros_like(y_cot))
        grad_down = jnp.einsum('mf,md->fd', hidden, g_out, preferred_element_type=jnp.float32)
        d_hidden = jnp.einsum('md,fd->mf', g_out, w_down, preferred_element_type=jnp.float32).astype(jnp.bfloat16)
        gelu_pull = jax.vjp(jax.nn.gelu, h_pre)[1]
        d_hpre = gelu_pull(d_hidden.astype(jnp.float32))[0].astype(jnp.bfloat16)
        grad_up = jnp.einsum('md,mf->df', z_mid, d_hpre, preferred_element_type=jnp.float32)
        d_z = (g_out.astype(jnp.float32) + jnp.einsum('mf,df->md', d_hpre, w_up, preferred_element_type=jnp.float32)).astype(jnp.bfloat16)
        d_pre = jnp.where(pre_act > 0, d_z, jnp.zeros_like(d_z))
        grad_self = jnp.einsum('md,me->de', x_feat, d_pre, preferred_element_type=jnp.float32)
        grad_msg = jnp.einsum('md,me->de', agg_msg, d_pre, preferred_element_type=jnp.float32)
        d_agg = jnp.einsum('me,de->md', d_pre, w_msg, preferred_element_type=jnp.float32).astype(jnp.bfloat16)
        d_table = jnp.einsum('ms,md->sd', adjacency, d_agg, preferred_element_type=jnp.float32)
        halo_back = deliver(d_table[rows_dev:].astype(jnp.bfloat16).reshape(nodes, -1, width), halo_got, rows_dev)

        d_u = serve(d_z, wanted).reshape(nodes * capacity, width)[route_ix]
        grad_o = jnp.einsum('md,me->de', mixed_rows, d_u, preferred_element_type=jnp.float32)
        d_mixed = jnp.einsum('me,de->md', d_u, w_o, preferred_element_type=jnp.float32).astype(jnp.bfloat16).reshape(rows_dev * heads, head_dim)
        delta = jnp.sum(d_mixed.astype(jnp.float32) * mixed.astype(jnp.float32), axis=1)
        dq_rows, dk_all, dv_all = attention_backward(q_rows, key_all, val_all, ok_all, scale, log_norm, d_mixed, delta)
        d_query = dq_rows.reshape(rows_dev, width).astype(jnp.bfloat16)
        d_key = lax.psum_scatter(dk_all, 'nodes', scatter_dimension=0, tiled=False).astype(jnp.bfloat16)
        d_value = lax.psum_scatter(dv_all, 'nodes', scatter_dimension=0, tiled=False).astype(jnp.bfloat16)
        grad_q = jnp.einsum('md,me->de', hidden_in, d_query, preferred_element_type=jnp.float32)
        grad_k = jnp.einsum('md,me->de', hidden_in, d_key, preferred_element_type=jnp.float32)
        grad_v = jnp.einsum('md,me->de', hidden_in, d_value, preferred_element_type=jnp.float32)
        dx_bal = (jnp.einsum('me,de->md', d_query, w_q, preferred_element_type=jnp.float32) + jnp.einsum('me,de->md', d_key, w_k, preferred_element_type=jnp.float32) + jnp.einsum('me,de->md', d_value, w_v, preferred_element_type=jnp.float32)).astype(jnp.bfloat16)
        attn_back = deliver(jnp.take(dx_bal, sources, axis=0).reshape(nodes, capacity, width), wanted, rows_dev)
        dx_feat = (2.0 * d_z.astype(jnp.float32) + jnp.einsum('me,de->md', d_pre, w_self, preferred_element_type=jnp.float32) + d_table[:rows_dev] + halo_back + attn_back).astype(jnp.bfloat16)
        grads = lax.psum((grad_msg, grad_self, grad_q, grad_k, grad_v, grad_o, grad_up, grad_down), 'nodes')
        return (y_out, dx_feat) + tuple(grads)

    return jax.shard_map(device_step, mesh=mesh, in_specs=(row_spec, flat_spec, halo_spec, row_spec, row_spec, row_spec, flat_spec, row_spec, row_spec) + (P(),) * 8, out_specs=(row_spec, row_spec) + (grad_spec,) * 8, check_vma=False)
```

profile of v0, /device:TPU:21, one launch (start us, length us, event | category | flops | bytes accessed | tf_op | source)
XLA Modules:
  0.0 1021.2 jit_solution(13472409086450007252)
XLA Ops:
  12.1 17.6 %all_to_all.57 = s32[16,1,48]{2,1,0:T(1,128)S(1)} all-to-all(s32[16,1,48]{2,1,0:T(1,128)S(1)} %all_to_all.39), channel_id=1, replica_groups=mesh['graphs'=4,'nodes'=16] {'nodes'}, dimensions={0} | all-to-all | bytes 6144 | tf_op jit(solution)/shard_map/all_to_all | solution.py:97
  31.0 4.5 gather_fusion.3
  35.5 4.2 all-to-all-start.4
  39.8 21.8 %all-to-all-done.4 = bf16[16,48,512]{2,1,0:T(8,128)(2,1)S(1)} async-done(((bf16[16,48,512]{2,1,0:T(8,128)(2,1)}), bf16[16,48,512]{2,1,0:T(8,128)(2,1)S(1)}, u32[]{:S(2)}, u32[]{:S(2)}) %all-to-all-start.4) | async-done | bytes 786464 | tf_op jit(solution)/shard_map/all_to_all | solution.py:11
  66.6 3.7 all-to-all-start
  80.2 5.0 gather_fusion.1
  85.9 7.1 all-to-all-start.3
  95.6 4.2 all-to-all-done.3
  99.9 4.6 all-to-all-start.1
  107.5 23.9 %all-gather.3 = s32[16,1,512]{2,1,0:T(1,128)S(1)} all-gather(s32[1,1,512]{2,1,0:T(1,128)S(1)} %bitcast.171), channel_id=2, replica_groups=mesh['graphs'=4,'nodes'=16] {'nodes'}, dimensions={0}, use_global_device_ids=true | all-gather | bytes 34816 | tf_op jit(solution)/shard_map/all_gather | solution.py:106
  141.5 143.1 %while.30 = (s32[]{:T(128)}, f32[4096]{0:T(1024)S(1)}, f32[4096]{0:T(1024)S(1)}, f32[4096,64]{0,1:T(8,128)}, s32[16,512]{1,0:T(8,128)S(1)}, /*index=5*/bf16[16,5...) while((s32[]{:T(128)}, f32[4096]{0:T(1024)S(1)}, ...), condition=%wide.region_8.9_spmd.clone, body=%wide.region_5.8_spmd.clone.sunk | while | flops 560747008 | bytes 37228732 | solution.py:51
  146.5 3.0 convolution_add_fusion.10
  155.4 3.0 convolution_add_fusion.10
  164.4 3.0 convolution_add_fusion.10
  173.3 3.0 convolution_add_fusion.10
  182.3 3.0 convolution_add_fusion.10
  191.2 3.0 convolution_add_fusion.10
  200.1 3.0 convolution_add_fusion.10
  209.1 3.0 convolution_add_fusion.10
  218.0 3.0 convolution_add_fusion.10
  227.0 3.0 convolution_add_fusion.10
  235.9 3.0 convolution_add_fusion.10
  244.9 3.0 convolution_add_fusion.10
  253.8 3.0 convolution_add_fusion.10
  262.8 3.0 convolution_add_fusion.10
  271.7 3.0 convolution_add_fusion.10
  280.6 3.0 convolution_add_fusion.10
  284.6 3.2 copy.44
  294.7 3.3 gather_fusion.7
  300.3 6.6 all-to-all-start.5
  308.3 135.6 %scatter_custom_fusion.5 = f32[524288]{0:T(1024)} fusion(s32[25600]{0:T(1024)} %broadcast_select_fusion.3, f32[25600]{0:T(1024)} %bitcast.167, f32[]{:T(128)} %constant.62.clone.1), kind=kCustom, calls=%fused_computation.112 | custom fusion | flops 25600 | bytes 2097664
  453.2 8.0 scatter_custom_fusion.2
  465.6 3.6 fusion.37
  471.4 3.3 gather_fusion.5
  474.8 7.4 all-to-all-start.7
  482.4 21.4 %all-to-all-done.7 = bf16[16,48,512]{2,1,0:T(8,128)(2,1)S(1)} async-done(((bf16[16,48,512]{2,1,0:T(8,128)(2,1)}), bf16[16,48,512]{2,1,0:T(8,128)(2,1)S(1)}, u32[]{:S(2)}, u32[]{:S(2)}) %all-to-all-start.7) | async-done | bytes 786464 | tf_op jit(solution)/shard_map/all_to_all | solution.py:11
  512.0 191.2 %while.31 = (s32[]{:T(128)}, f32[4096,64]{0,1:T(8,128)}, f32[16,512,64]{1,2,0:T(8,128)}, f32[16,512,64]{1,2,0:T(8,128)}, s32[16,512]{1,0:T(8,128)}, /*index=5*/b...) while((s32[]{:T(128)}, f32[4096,64]{0,1:T(8,128)}, ...), condition=%wide.region_14.16_spmd.clone, body=%wide.region_13.15_spmd.clone.sunk | while | flops 1357382144 | bytes 51023068 | solution.py:69
  524.7 2.8 subtract_exponential_fusion.5
  536.7 2.8 subtract_exponential_fusion.5
  560.6 2.8 subtract_exponential_fusion.5
  572.5 2.8 subtract_exponential_fusion.5
  596.4 2.8 subtract_exponential_fusion.5
  608.3 2.8 subtract_exponential_fusion.5
  620.3 2.8 subtract_exponential_fusion.5
  632.2 2.8 subtract_exponential_fusion.5
  644.2 2.8 subtract_exponential_fusion.5
  668.1 2.8 subtract_exponential_fusion.5
  680.0 2.8 subtract_exponential_fusion.5
  692.0 2.8 subtract_exponential_fusion.5
  703.3 3.3 broadcast_multiply_fusion
  709.8 3.3 fusion.96
  713.2 3.8 fusion.89
  725.0 30.1 %reduce-scatter.5.cloned.1.call-done = f32[1,512,64]{1,2,0:T(8,128)} async-done(((f32[16,512,64]{1,2,0:T(8,128)}), f32[1,512,64]{1,2,0:T(8,128)}) %reduce-scatter.5.cloned.1.call-update) | async-done | bytes 131088 | tf_op jit(solution)/shard_map/reduce_scatter | solution.py:140
  756.8 55.7 %reduce-scatter.3.cloned.1.call-done = f32[1,512,64]{1,2,0:T(8,128)} async-done(((f32[16,512,64]{1,2,0:T(8,128)}), f32[1,512,64]{1,2,0:T(8,128)}) %reduce-scatter.3.cloned.1.call-update) | async-done | bytes 131088 | tf_op jit(solution)/shard_map/reduce_scatter | solution.py:139
  815.7 3.5 fusion.57
  821.3 8.0 all-to-all-start.6
  834.3 14.4 %all-to-all-done.6 = bf16[16,32,512]{2,1,0:T(8,128)(2,1)} async-done(((bf16[16,32,512]{2,1,0:T(8,128)(2,1)}), bf16[16,32,512]{2,1,0:T(8,128)(2,1)}, u32[]{:S(2)}, u32[]{:S(2)}) %all-to-all-start.6) | async-done | bytes 524320 | tf_op jit(solution)/shard_map/all_to_all | solution.py:15
  848.7 4.9 all-to-all-start.8
  853.7 5.2 fusion.53
  858.8 4.4 scatter_custom_fusion.3
  863.2 16.1 %all-to-all-done.8 = bf16[16,48,512]{2,1,0:T(8,128)(2,1)} async-done(((bf16[16,48,512]{2,1,0:T(8,128)(2,1)}), bf16[16,48,512]{2,1,0:T(8,128)(2,1)}, u32[]{:S(2)}, u32[]{:S(2)}) %all-to-all-start.8) | async-done | bytes 786464 | tf_op jit(solution)/shard_map/all_to_all | solution.py:15
  879.4 8.2 scatter_custom_fusion.4
  887.6 2.9 fusion.54
  890.5 109.7 %all-reduce.3.cloned.1.call-done = (f32[512,512]{1,0:T(8,128)}, f32[512,512]{0,1:T(8,128)}, f32[512,512]{1,0:T(8,128)}, f32[512,64]{0,1:T(8,128)}, f32[512,64]{0...) async-done(((f32[512,512]{1,0:T(8,128)}, f32[512,512]{0,1:T(8,128)}, f32[512,512]{1,0:T(8,128)}, f32[512,64]{0,1:T(8,128)}, ...) | async-done | bytes 12845072 | tf_op jit(solution)/shard_map/psum | solution.py:147
  (511 shorter events, 360.6 us)
Async XLA Ops:
  7.2 457.1 %copy-start = (bf16[512,2048]{1,0:T(8,128)(2,1)S(1)}, bf16[512,2048]{1,0:T(8,128)(2,1)}, u32[]{:S(2)}) copy-start(bf16[512,2048]{1,0:T(8,128)(2,1)} %param.38) | copy-start | bytes 6291460
  31.0 4.5 copy-start.47
  35.5 30.1 %copy-start.39 = (bf16[512,64]{0,1:T(8,128)(2,1)S(1)}, bf16[512,64]{0,1:T(8,128)(2,1)}, u32[]{:S(2)}) copy-start(bf16[512,64]{0,1:T(8,128)(2,1)} %param.35) | copy-start | bytes 196612
  35.5 34.9 %copy-start.37 = (bf16[512,64]{0,1:T(8,128)(2,1)S(1)}, bf16[512,64]{0,1:T(8,128)(2,1)}, u32[]{:S(2)}) copy-start(bf16[512,64]{0,1:T(8,128)(2,1)} %param.36) | copy-start | bytes 196612
  35.5 26.1 %all-to-all-start.4 = ((bf16[16,48,512]{2,1,0:T(8,128)(2,1)}), bf16[16,48,512]{2,1,0:T(8,128)(2,1)S(1)}, u32[]{:S(2)}, u32[]{:S(2)}) async-start(bf16[16,48,512]{2,1,0:T(8,128)(2,1)} %bitcast.162), calls=%async_computation.4 | async-start | bytes 1572864 | tf_op jit(solution)/shard_map/all_to_all | solution.py:11
  39.7 96.4 %all-gather.7.cloned.1.call-start = ((), (), s32[]{:S(2)}) async-start(), calls=%async_computation.13 | async-start | bytes 1114112 | tf_op jit(solution)/shard_map/all_gather | solution.py:104
  39.8 35.2 %copy-start.44 = (s32[1024]{0:T(1024)}, s32[1024]{0:T(1024)S(1)}, u32[]{:S(2)}) copy-start(s32[1024]{0:T(1024)S(1)} %pad_clamp_fusion.1) | copy-start | bytes 12292
  61.6 18.6 %copy-start.2 = (s32[512]{0:T(512)S(1)}, s32[512]{0:T(512)}, u32[]{:S(2)}) copy-start(s32[512]{0:T(512)} %param.24) | copy-start | bytes 6148
  64.2 28.8 %copy-start.3 = (bf16[512,512]{1,0:T(8,128)(2,1)S(1)}, bf16[512,512]{1,0:T(8,128)(2,1)}, u32[]{:S(2)}) copy-start(bf16[512,512]{1,0:T(8,128)(2,1)} %param.23) | copy-start | bytes 1572868
  65.6 65.9 %copy-start.8 = (bf16[512,512]{1,0:T(8,128)(2,1)}, bf16[512,512]{1,0:T(8,128)(2,1)S(1)}, u32[]{:S(2)}) copy-start(bf16[512,512]{1,0:T(8,128)(2,1)S(1)} %add_convert_fusion) | copy-start | bytes 1572868
  66.6 12.9 %all-to-all-start = ((s32[16,1,32]{2,1,0:T(1,128)}), s32[16,1,32]{2,1,0:T(1,128)S(1)}, u32[]{:S(2)}, u32[]{:S(2)}) async-start(s32[16,1,32]{2,1,0:T(1,128)} %bitcast.170), calls=%async_computation | async-start | bytes 16384 | tf_op jit(solution)/shard_map/all_to_all | solution.py:89
  70.3 68.6 %all-gather.9.cloned.1.call-start = ((), (), s32[]{:S(2)}) async-start(), calls=%async_computation.14 | async-start | bytes 1114112 | tf_op jit(solution)/shard_map/all_gather | solution.py:105
  77.8 220.3 %copy-start.48 = (pred[768]{0:T(1024)(128)(4,1)}, pred[768]{0:T(1024)(128)(4,1)S(1)}, u32[]{:S(2)}) copy-start(pred[768]{0:T(1024)(128)(4,1)S(1)} %compare_and_fusion) | copy-start | bytes 2308
  80.2 15.4 %copy-start.50 = (s32[512]{0:T(512)}, s32[512]{0:T(512)S(1)}, u32[]{:S(2)}) copy-start(s32[512]{0:T(512)S(1)} %reshape.229) | copy-start | bytes 6148
  80.2 25.1 %copy-start.45 = (s32[1024]{0:T(1024)S(1)}, s32[1024]{0:T(1024)}, u32[]{:S(2)}) copy-start(s32[1024]{0:T(1024)} %copy-done.44) | copy-start | bytes 12292
  85.9 14.0 %all-to-all-start.3 = ((s32[16,1,48]{2,1,0:T(1,128)}), s32[16,1,48]{2,1,0:T(1,128)S(1)}, u32[]{:S(2)}, u32[]{:S(2)}) async-start(s32[16,1,48]{2,1,0:T(1,128)} %all_to_all.41), calls=%async_computation.3 | async-start | bytes 16384 | tf_op jit(solution)/shard_map/all_to_all | solution.py:11
  99.9 200.4 %all-to-all-start.1 = ((bf16[16,32,512]{2,1,0:T(8,128)(2,1)}), bf16[16,32,512]{2,1,0:T(8,128)(2,1)}, u32[]{:S(2)}, u32[]{:S(2)}) async-start(bf16[16,32,512]{2,1,0:T(8,128)(2,1)} %bitcast.166), calls=%async_computation.1 | async-start | bytes 1048576 | tf_op jit(solution)/shard_map/all_to_all | solution.py:11
  284.6 10.1 copy-start.43
  300.3 153.0 %all-to-all-start.5 = ((bf16[16,48,512]{2,1,0:T(8,128)(2,1)}), bf16[16,48,512]{2,1,0:T(8,128)(2,1)S(1)}, u32[]{:S(2)}, u32[]{:S(2)}) async-start(bf16[16,48,512]{2,1,0:T(8,128)(2,1)} %bitcast.164), calls=%async_computation.5 | async-start | bytes 1572864 | tf_op jit(solution)/shard_map/all_to_all | solution.py:15
  448.9 2.9 copy-start.36
  465.6 3.7 copy-start.20
  471.4 32.4 %copy-start.46 = (s32[1024]{0:T(1024)S(1)}, s32[1024]{0:T(1024)}, u32[]{:S(2)}) copy-start(s32[1024]{0:T(1024)} %copy-done.44) | copy-start | bytes 12292
  474.8 31.8 %copy-start.22 = (bf16[512,512]{1,0:T(8,128)(2,1)S(1)}, bf16[512,512]{1,0:T(8,128)(2,1)}, u32[]{:S(2)}) copy-start(bf16[512,512]{1,0:T(8,128)(2,1)} %param.37) | copy-start | bytes 1572868
  474.8 29.1 %all-to-all-start.7 = ((bf16[16,48,512]{2,1,0:T(8,128)(2,1)}), bf16[16,48,512]{2,1,0:T(8,128)(2,1)S(1)}, u32[]{:S(2)}, u32[]{:S(2)}) async-start(bf16[16,48,512]{2,1,0:T(8,128)(2,1)} %bitcast.15), calls=%async_computation.7 | async-start | bytes 1572864 | tf_op jit(solution)/shard_map/all_to_all | solution.py:11
  482.1 272.9 %reduce-scatter.5.cloned.1.call-start = ((), (), s32[]{:S(2)}) async-start(), calls=%async_computation.12 | async-start | bytes 2228224 | tf_op jit(solution)/shard_map/reduce_scatter | solution.py:140
  506.6 5.4 copy-start.4
  517.7 2.3 copy-start.5
  529.6 2.3 copy-start.5
  541.5 2.3 copy-start.5
  553.5 2.3 copy-start.5
  565.4 2.3 copy-start.5
  589.3 2.3 copy-start.5
  601.3 2.3 copy-start.5
  613.2 2.3 copy-start.5
  672.9 2.3 copy-start.5
  703.2 3.8 copy-start.13
  703.2 3.8 copy-start.28
  703.2 109.3 %reduce-scatter.3.cloned.1.call-start = ((), (), s32[]{:S(2)}) async-start(), calls=%async_computation.11 | async-start | bytes 2228224 | tf_op jit(solution)/shard_map/reduce_scatter | solution.py:139
  706.6 3.2 copy-start.16
  706.6 293.5 %all-reduce.3.cloned.1.call-start = ((), (), s32[]{:S(2)}) async-start(), calls=%async_computation.15 | async-start | bytes 25690112 | tf_op jit(solution)/shard_map/psum | solution.py:147
  706.9 2.9 copy-start.25
  708.4 4.8 copy-start.21
  708.4 4.8 copy-start.53
  713.2 3.8 copy-start.7
  717.0 5.1 copy-start.10
  717.0 5.1 copy-start.12
  717.0 6.6 copy-start.9
  815.7 13.6 %copy-start.26 = (bf16[512,512]{1,0:T(8,128)(2,1)S(1)}, bf16[512,512]{1,0:T(8,128)(2,1)}, u32[]{:S(2)}) copy-start(bf16[512,512]{1,0:T(8,128)(2,1)} %param.34) | copy-start | bytes 1572868
  815.7 14.1 %copy-start.35 = (f32[1,512,64]{1,2,0:T(8,128)S(1)}, f32[1,512,64]{1,2,0:T(8,128)}, u32[]{:S(2)}) copy-start(f32[1,512,64]{1,2,0:T(8,128)} %reduce-scatter.3.cloned.1.call-done) | copy-start | bytes 393220
  815.7 14.1 %copy-start.40 = (bf16[512,64]{0,1:T(8,128)(2,1)S(1)}, bf16[512,64]{0,1:T(8,128)(2,1)}, u32[]{:S(2)}) copy-start(bf16[512,64]{0,1:T(8,128)(2,1)} %param.35) | copy-start | bytes 196612
  819.2 11.0 %copy-start.34 = (f32[1,512,64]{1,2,0:T(8,128)S(1)}, f32[1,512,64]{1,2,0:T(8,128)}, u32[]{:S(2)}) copy-start(f32[1,512,64]{1,2,0:T(8,128)} %reduce-scatter.5.cloned.1.call-done) | copy-start | bytes 393220
  819.2 11.0 %copy-start.38 = (bf16[512,64]{0,1:T(8,128)(2,1)S(1)}, bf16[512,64]{0,1:T(8,128)(2,1)}, u32[]{:S(2)}) copy-start(bf16[512,64]{0,1:T(8,128)(2,1)} %param.36) | copy-start | bytes 196612
  821.3 27.4 %all-to-all-start.6 = ((bf16[16,32,512]{2,1,0:T(8,128)(2,1)}), bf16[16,32,512]{2,1,0:T(8,128)(2,1)}, u32[]{:S(2)}, u32[]{:S(2)}) async-start(bf16[16,32,512]{2,1,0:T(8,128)(2,1)} %bitcast.13), calls=%async_computation.6 | async-start | bytes 1048576 | tf_op jit(solution)/shard_map/all_to_all | solution.py:15
  830.2 3.0 copy-start.49
  830.5 23.1 %copy-start.17 = (bf16[512,512]{1,0:T(8,128)(2,1)S(1)}, bf16[512,512]{1,0:T(8,128)(2,1)}, u32[]{:S(2)}) copy-start(bf16[512,512]{1,0:T(8,128)(2,1)} %copy-done.15) | copy-start | bytes 1572868
  848.7 30.7 %all-to-all-start.8 = ((bf16[16,48,512]{2,1,0:T(8,128)(2,1)}), bf16[16,48,512]{2,1,0:T(8,128)(2,1)}, u32[]{:S(2)}, u32[]{:S(2)}) async-start(bf16[16,48,512]{2,1,0:T(8,128)(2,1)} %bitcast.165), calls=%async_computation.10 | async-start | bytes 1572864 | tf_op jit(solution)/shard_map/all_to_all | solution.py:15
  853.6 34.0 %copy-start.23 = (bf16[512,512]{1,0:T(8,128)(2,1)S(1)}, bf16[512,512]{1,0:T(8,128)(2,1)}, u32[]{:S(2)}) copy-start(bf16[512,512]{1,0:T(8,128)(2,1)} %param.33) | copy-start | bytes 1572868
  1000.2 5.1 copy-start.33
  1000.2 6.1 copy-start.42
  1000.2 6.7 copy-start.41
  1000.2 7.4 copy-start.32
  1002.9 5.7 copy-start.19
  1008.5 3.7 copy-start.18
  1008.5 5.7 copy-start.1
  (63 other events, 110.6 us)
Sparse Core Ops, SparseCore 0:
  66.7 33.2 all-gather.6
  102.2 34.9 all-gather.8
  703.4 51.6 reduce-scatter.4
  757.3 55.2 reduce-scatter.2
  816.5 183.5 all-reduce.2
where the time goes:
time: 1030 us; the launch traced here: 1020 us
  matrix products  320 us (31%)
  waiting for transfers between devices  274 us (27%)
  other arithmetic  230 us (22%)
  local copies, waits for them, and re-layouts  92.2 us (9%)
  starting transfers between devices  47.2 us (5%)
  blocking collectives  41.5 us (4%)
  between operations  14.9 us (1%)
    unnamed x8, other arithmetic  140 us
    psum x1, waiting for transfers between devices, device_step(): lax.psum((grad_msg, grad_self, grad_q, grad_k, grad_v, grad_o, grad_up, g...  110 us
    dot_general x32, matrix products, shard_step(): jnp.einsum('qe,ke->qk', q_rows, key_blk, preferred_element_type=jnp.float32)  89 us
    reduce_scatter x1, waiting for transfers between devices, device_step(): lax.psum_scatter(dk_all, 'nodes', scatter_dimension=0, tiled=False)  55.7 us
    dot_general x16, matrix products, shard_step(): jnp.dot(prob_blk.astype(jnp.bfloat16), val_blk, preferred_element_type=jn...  47.9 us
    all_to_all x4, waiting for transfers between devices, serve(): lax.all_to_all(picked.reshape(wanted.shape + source.shape[1:]), 'nodes',...  47.4 us
    dot_general x16, matrix products, shard_step(): jnp.einsum('qe,ke->qk', d_mixed, val_blk, preferred_element_type=jnp.floa...  36.8 us
    reduce_sum x16, other arithmetic, shard_step(): run_sum = run_sum * decay + jnp.sum(prob_blk, axis=1)  33.5 us
  transfers between devices with their start and end apart: 13, of which 8 were waited for; matrix products, arithmetic and copies ran while one was open for 36% of the time, Pallas kernels for 0%

commit v1 on v0

v1 whole, which is shorter than its diff:
```python
import functools
import jax
import jax.numpy as jnp
from jax import lax
from jax.experimental import pallas as pl
from jax.experimental.pallas import tpu as pltpu
from jax.sharding import PartitionSpec as P

F32 = jnp.float32
BF16 = jnp.bfloat16
NEG_FILL = -1e30
LANES = 128
MESH = pl.DeviceIdType.MESH


def dot(a, b, ca, cb):
    return lax.dot_general(a, b, (((ca,), (cb,)), ((), ())), preferred_element_type=F32)


def adjacency_kernel(src_ref, dst_ref, out_ref, acc_ref):
    rows, cols = out_ref.shape
    steps, chunk = src_ref.shape
    acc_ref[...] = jnp.zeros_like(acc_ref)
    dst_iota = lax.broadcasted_iota(jnp.int32, (rows, chunk), 0)
    src_iota = lax.broadcasted_iota(jnp.int32, (cols, chunk), 0)

    def body(i, c):
        left = jnp.where(dst_iota == dst_ref[pl.ds(i, 1), :], 1.0, 0.0).astype(BF16)
        right = jnp.where(src_iota == src_ref[pl.ds(i, 1), :], 1.0, 0.0).astype(BF16)
        acc_ref[...] += dot(left, right, 1, 1)
        return c

    lax.fori_loop(0, steps, body, 0)
    out_ref[...] = acc_ref[...].astype(BF16)


def build_adjacency(edge_src, edge_dst, rows, cols, chunk=2560):
    edges = edge_src.size
    if edges % chunk:
        chunk = LANES
    steps = edges // chunk
    return pl.pallas_call(
        adjacency_kernel,
        out_shape=jax.ShapeDtypeStruct((rows, cols), BF16),
        scratch_shapes=[pltpu.VMEM((rows, cols), F32)],
        cost_estimate=pl.CostEstimate(flops=2 * edges * rows * cols, bytes_accessed=2 * rows * cols, transcendentals=0),
        name='adjacency',
    )(edge_src.reshape(steps, chunk), edge_dst.reshape(steps, chunk))


def forward_kernel(k_ref, vt_ref, q_ref, o_ref, lse_ref, *, blocks, group, unroll):
    rows = q_ref.shape[1]
    head_dim = o_ref.shape[0]
    part = vt_ref.shape[2]
    bk = part * group
    q = q_ref[...]

    def body(j, carry):
        run_max, run_sum, acc = carry
        start = pl.multiple_of(j * bk, bk)
        scores = dot(k_ref[pl.ds(start, bk), :], q, 1, 0)
        new_max = jnp.maximum(run_max, jnp.max(scores, axis=0, keepdims=True))
        prob = jnp.exp(scores - new_max)
        decay = jnp.exp(run_max - new_max)
        run_sum = run_sum * decay + jnp.sum(prob, axis=0, keepdims=True)
        prob = prob.astype(BF16)
        acc = acc * decay
        for g in range(group):
            acc = acc + dot(vt_ref[j * group + g, :head_dim, :], prob[g * part:(g + 1) * part], 1, 0)
        return new_max, run_sum, acc

    init = (jnp.full((1, rows), -jnp.inf, F32), jnp.zeros((1, rows), F32), jnp.zeros((head_dim, rows), F32))
    run_max, run_sum, acc = lax.fori_loop(0, blocks, body, init, unroll=unroll)
    o_ref[...] = (acc / run_sum).astype(BF16)
    lse_ref[0] = run_max + jnp.log(run_sum)


def attention_forward(k_ext, vt_ext, qt_ext, heads, head_dim, group=4, unroll=2):
    keys = k_ext.shape[0]
    rows = qt_ext.shape[1]
    nodes, wide, part = vt_ext.shape
    return pl.pallas_call(
        functools.partial(forward_kernel, blocks=nodes // group, group=group, unroll=unroll),
        grid=(heads,),
        in_specs=[
            pl.BlockSpec((keys, LANES), lambda h: (0, 0)),
            pl.BlockSpec((nodes, wide, part), lambda h: (0, 0, 0)),
            pl.BlockSpec((LANES, rows), lambda h: (h, 0)),
        ],
        out_specs=[pl.BlockSpec((head_dim, rows), lambda h: (h, 0)), pl.BlockSpec((1, 1, rows), lambda h: (h, 0, 0))],
        out_shape=[jax.ShapeDtypeStruct((heads * head_dim, rows), BF16), jax.ShapeDtypeStruct((heads, 1, rows), F32)],
        compiler_params=pltpu.CompilerParams(vmem_limit_bytes=56 * 2**20),
        cost_estimate=pl.CostEstimate(flops=4 * heads * rows * keys * head_dim, bytes_accessed=2**23, transcendentals=heads * rows * keys),
        name='attention_forward',
    )(k_ext, vt_ext, qt_ext)


def backward_kernel(kt_ref, vt_ref, q_ref, do_ref, qt_ref, dot_ref, dkv_ref, dq_ref, sums, send_sem, recv_sem, *, nodes, heads, head_dim, unroll):
    bk = kt_ref.shape[-1]
    me = lax.axis_index('nodes')
    right, left = lax.rem(me + 1, nodes), lax.rem(me + nodes - 1, nodes)
    barrier = pltpu.get_barrier_semaphore()
    for neighbour in (left, right):
        pl.semaphore_signal(barrier, inc=1, device_id={'nodes': neighbour}, device_id_type=MESH)
    pl.semaphore_wait(barrier, 2)
    dq_ref[...] = jnp.zeros_like(dq_ref)

    def hop(t):
        return pltpu.make_async_remote_copy(src_ref=sums.at[t], dst_ref=sums.at[t + 1], send_sem=send_sem.at[t], recv_sem=recv_sem.at[t + 1], device_id={'nodes': right}, device_id_type=MESH)

    def step(t, c):
        j = lax.rem(me + 2 * nodes - 1 - t, nodes)
        kt = kt_ref[j]
        vt = vt_ref[j]
        k_top = kt[:head_dim]

        def body(h, carry):
            dk, dv = carry
            lo = pl.multiple_of(h * LANES, LANES)
            r0 = pl.multiple_of(h * head_dim, head_dim)
            prob = jnp.exp(dot(q_ref[:, pl.ds(lo, LANES)], kt, 1, 0))
            d_prob = dot(do_ref[:, pl.ds(lo, LANES)], vt, 1, 0)
            d_scores = (prob * d_prob).astype(BF16)
            dv = dv + dot(dot_ref[pl.ds(r0, head_dim), :], prob.astype(BF16), 1, 0)
            dk = dk + dot(qt_ref[pl.ds(lo, head_dim), :], d_scores, 1, 0)
            dq_ref[pl.ds(r0, head_dim), :] += dot(k_top, d_scores, 1, 1)
            return dk, dv

        zero = jnp.zeros((head_dim, bk), F32)
        dk, dv = lax.fori_loop(0, heads, body, (zero, zero), unroll=unroll)

        @pl.when(t == 0)
        def _():
            sums[t, :head_dim, :] = dk
            sums[t, head_dim:, :] = dv

        @pl.when(t > 0)
        def _():
            hop(t - 1).wait_recv()
            sums[t, :head_dim, :] += dk
            sums[t, head_dim:, :] += dv

        @pl.when(t < nodes - 1)
        def _():
            hop(t).start()
        return c

    lax.fori_loop(0, nodes, step, 0)

    def finish(t, c):
        hop(t).wait_send()
        return c

    lax.fori_loop(0, nodes - 1, finish, 0)
    dkv_ref[...] = sums[nodes - 1].astype(BF16)


def attention_backward(kt_ext, vt_ext, q_ext, do_ext, qt_ext, do_t, heads, head_dim, unroll=4):
    nodes, wide, bk = kt_ext.shape
    rows = q_ext.shape[0]
    return pl.pallas_call(
        functools.partial(backward_kernel, nodes=nodes, heads=heads, head_dim=head_dim, unroll=unroll),
        in_specs=[pl.BlockSpec(memory_space=pltpu.VMEM)] * 6,
        out_specs=[pl.BlockSpec(memory_space=pltpu.VMEM)] * 2,
        out_shape=[jax.ShapeDtypeStruct((2 * head_dim, bk), BF16), jax.ShapeDtypeStruct((heads * head_dim, rows), F32)],
        scratch_shapes=[pltpu.VMEM((nodes, 2 * head_dim, bk), F32), pltpu.SemaphoreType.DMA((nodes,)), pltpu.SemaphoreType.DMA((nodes,))],
        compiler_params=pltpu.CompilerParams(vmem_limit_bytes=40 * 2**20, collective_id=0, has_side_effects=True),
        cost_estimate=pl.CostEstimate(flops=10 * heads * rows * nodes * bk * head_dim, bytes_accessed=2**24, transcendentals=heads * rows * nodes * bk),
        name='attention_backward',
    )(kt_ext, vt_ext, q_ext, do_ext, qt_ext, do_t)


def reduce_kernel(x_ref, out_ref, half, parts, pair_send, pair_recv, part_send, part_recv, full_send, full_recv, back_send, back_recv, *, nodes):
    me = lax.axis_index('nodes')
    chips = nodes // 2
    core = lax.rem(me, 2)
    chip = me // 2
    partner = me + 1 - 2 * core
    rows = x_ref.shape[0]
    hr = rows // 2
    pr = hr // chips
    mine = pl.multiple_of(core * hr, hr)
    other = pl.multiple_of((1 - core) * hr, hr)

    def peer(k):
        return lax.rem(chip + k, chips)

    barrier = pltpu.get_barrier_semaphore()
    pl.semaphore_signal(barrier, inc=1, device_id={'nodes': partner}, device_id_type=MESH)
    for k in range(1, chips):
        pl.semaphore_signal(barrier, inc=1, device_id={'nodes': 2 * peer(k) + core}, device_id_type=MESH)
    pl.semaphore_wait(barrier, chips)

    swap = pltpu.make_async_remote_copy(src_ref=x_ref.at[pl.ds(other, hr)], dst_ref=half, send_sem=pair_send, recv_sem=pair_recv, device_id={'nodes': partner}, device_id_type=MESH)
    swap.start()
    swap.wait_recv()
    half[...] += x_ref[pl.ds(mine, hr)]

    def scatter(k):
        to = peer(k)
        return pltpu.make_async_remote_copy(src_ref=half.at[pl.ds(pl.multiple_of(to * pr, pr), pr)], dst_ref=parts.at[k], send_sem=part_send.at[k], recv_sem=part_recv.at[k], device_id={'nodes': 2 * to + core}, device_id_type=MESH)

    for k in range(1, chips):
        scatter(k).start()
    total = half[pl.ds(pl.multiple_of(chip * pr, pr), pr)]
    for k in range(1, chips):
        scatter(k).wait_recv()
        total = total + parts[k]
    own = pl.multiple_of(core * hr + chip * pr, pr)
    out_ref[pl.ds(own, pr)] = total

    def spread(k):
        return pltpu.make_async_remote_copy(src_ref=out_ref.at[pl.ds(own, pr)], dst_ref=out_ref.at[pl.ds(own, pr)], send_sem=full_send.at[k], recv_sem=full_recv.at[k], device_id={'nodes': 2 * peer(k) + core}, device_id_type=MESH)

    def back(k):
        at = pl.multiple_of(core * hr + lax.rem(chip + chips - k, chips) * pr, pr)
        return pltpu.make_async_remote_copy(src_ref=out_ref.at[pl.ds(at, pr)], dst_ref=out_ref.at[pl.ds(at, pr)], send_sem=back_send.at[k], recv_sem=back_recv.at[k], device_id={'nodes': partner}, device_id_type=MESH)

    for k in range(1, chips):
        spread(k).start()
    back(0).start()
    for k in range(1, chips):
        spread(k).wait_recv()
        back(k).start()
    for k in range(chips):
        back(k).wait_recv()
    swap.wait_send()
    for k in range(1, chips):
        scatter(k).wait_send()
        spread(k).wait_send()
    for k in range(chips):
        back(k).wait_send()


def reduce_all(x, nodes):
    rows, cols = x.shape
    chips = nodes // 2
    pr = rows // nodes
    sems = lambda: pltpu.SemaphoreType.DMA((chips,))
    return pl.pallas_call(
        functools.partial(reduce_kernel, nodes=nodes),
        in_specs=[pl.BlockSpec(memory_space=pltpu.VMEM)],
        out_specs=pl.BlockSpec(memory_space=pltpu.VMEM),
        out_shape=jax.ShapeDtypeStruct(x.shape, F32),
        scratch_shapes=[pltpu.VMEM((rows // 2, cols), F32), pltpu.VMEM((chips, pr, cols), F32), pltpu.SemaphoreType.DMA, pltpu.SemaphoreType.DMA, sems(), sems(), sems(), sems(), sems(), sems()],
        compiler_params=pltpu.CompilerParams(vmem_limit_bytes=16 * 2**20, collective_id=1, has_side_effects=True),
        cost_estimate=pl.CostEstimate(flops=10**10, bytes_accessed=2**23, transcendentals=0),
        name='reduce_all',
    )(x)


def one_hot(index, size):
    return (lax.broadcasted_iota(jnp.int32, (size, index.size), 0) == index[None, :]).astype(BF16)


def exchange(rows, send_ix, recv_ix, nodes):
    count, width = rows.shape
    capacity = count // nodes + count // (2 * nodes)
    picked = dot(one_hot(send_ix, nodes * capacity), rows, 1, 0).astype(BF16)
    landed = lax.all_to_all(picked.reshape(nodes, capacity, width), 'nodes', 0, 0, tiled=True)
    return dot(one_hot(recv_ix, nodes * capacity), landed.reshape(nodes * capacity, width), 0, 0).astype(BF16)


def routes(bal_perm, bal_all, rows_dev, nodes):
    capacity = rows_dev // nodes + rows_dev // (2 * nodes)
    before = (lax.broadcasted_iota(jnp.int32, (rows_dev, rows_dev), 0) < lax.broadcasted_iota(jnp.int32, (rows_dev, rows_dev), 1))
    owner = bal_perm // rows_dev
    same = owner[:, None] == owner[None, :]
    bal_ix = owner * capacity + jnp.sum((same & before).astype(jnp.int32), axis=0)
    me = lax.axis_index('nodes')
    mine = (bal_all // rows_dev == me).astype(BF16)
    rank = dot(mine, before.astype(BF16), 1, 0).astype(jnp.int32)
    code = lax.broadcasted_iota(jnp.int32, rank.shape, 0) * capacity + rank
    wanted = me * rows_dev + jnp.arange(rows_dev, dtype=jnp.int32)
    hit = bal_all.reshape(-1)[:, None] == wanted[None, :]
    part_ix = jnp.sum(jnp.where(hit, code.reshape(-1)[:, None], 0), axis=0)
    return bal_ix, part_ix


def split3(x):
    keep = lambda a: lax.reduce_precision(a, 8, 7)
    hi = keep(x)
    mid = keep(x - hi)
    return jnp.concatenate([hi, mid, keep(x - hi - mid)], axis=0).astype(BF16)


def pad_heads(w, heads, axis):
    if axis == 1:
        w3 = w.reshape(w.shape[0], heads, -1)
        return jnp.pad(w3, ((0, 0), (0, 0), (0, LANES - w3.shape[2]))).reshape(w.shape[0], heads * LANES)
    w3 = w.reshape(heads, -1, w.shape[1])
    return jnp.pad(w3, ((0, 0), (0, LANES - w3.shape[1]), (0, 0))).reshape(heads * LANES, w.shape[1])


def extra_columns(parts, heads, first):
    r = lax.broadcasted_iota(jnp.int32, (3 * heads, heads * LANES), 0)
    c = lax.broadcasted_iota(jnp.int32, (3 * heads, heads * LANES), 1)
    place = (r % heads == c // LANES) & (c % LANES == first + r // heads)
    return dot(parts, place.astype(BF16), 0, 0)


def solution(mesh):
    nodes = mesh.shape['nodes']
    row_spec = P(('graphs', 'nodes'), None)
    flat_spec = P(('graphs', 'nodes'))
    halo_spec = P(('graphs', 'nodes'), None, None)
    grad_spec = P('graphs', None)

    def device_step(x_feat, valid, halo_slot, edge_src, edge_dst, edge_mask, bal_perm, pos_enc, y_cot, w_msg, w_self, w_q, w_k, w_v, w_o, w_up, w_down):
        rows_dev, width = x_feat.shape
        head_dim = w_k.shape[1]
        heads = width // head_dim
        scale = head_dim ** -0.5
        me = lax.axis_index('nodes')
        halo_req = halo_slot.reshape(-1)
        halo_rows = halo_req.size

        count = jnp.sum((valid > 0).astype(jnp.int32))
        info = lax.all_gather(jnp.concatenate([bal_perm, halo_req, jnp.broadcast_to(count, (LANES,))]), 'nodes')
        bal_all = info[:, :rows_dev]
        halo_all = info[:, rows_dev:rows_dev + halo_rows].reshape(nodes, nodes, -1)
        count_all = info[:, rows_dev + halo_rows]
        bal_ix, part_ix = routes(bal_perm, bal_all, rows_dev, nodes)
        owner_all = bal_all // rows_dev
        limit = jnp.sum(jnp.where(owner_all[:, :, None] == jnp.arange(nodes, dtype=jnp.int32), count_all[None, None, :], 0), axis=2)
        key_bias = jnp.where(bal_all % rows_dev < limit, 0.0, NEG_FILL).astype(BF16)

        x_bal = exchange(x_feat, part_ix, bal_ix, nodes)
        hidden_in = (x_bal.astype(F32) + pos_enc.astype(F32)).astype(BF16)
        w_kv = jnp.concatenate([w_k, w_v], axis=1)
        kv_t = dot(w_kv, hidden_in, 0, 1).astype(BF16)
        kv_all = lax.all_gather(kv_t, 'nodes')
        wq_pad = pad_heads((w_q.astype(F32) * scale).astype(BF16), heads, 1)
        row_one = (lax.broadcasted_iota(jnp.int32, (heads * LANES, 1), 0) % LANES == head_dim).astype(F32)
        qt_ext = (dot(wq_pad, hidden_in, 0, 1) + row_one).astype(BF16)

        halo_got = lax.dynamic_index_in_dim(halo_all, me, axis=1, keepdims=False).reshape(-1)
        halo_pick = one_hot(halo_got, rows_dev)
        halo_send = dot(halo_pick, x_feat, 0, 0).astype(BF16)
        halo_feat = lax.all_to_all(halo_send.reshape(nodes, -1, width), 'nodes', 0, 0, tiled=True).reshape(halo_rows, width)
        live_dst = jnp.where(edge_mask.reshape(-1) > 0, edge_dst.reshape(-1), -1)
        adjacency = build_adjacency(edge_src.reshape(-1), live_dst, rows_dev, rows_dev + halo_rows)
        adj_own, adj_halo = adjacency[:, :rows_dev], adjacency[:, rows_dev:]
        agg_msg = (dot(adj_own, x_feat, 1, 0) + dot(adj_halo, halo_feat, 1, 0)).astype(BF16)
        pre_act = dot(agg_msg, w_msg, 1, 0) + dot(x_feat, w_self, 1, 0)

        wide = lambda n: (nodes, n, rows_dev)
        ones3 = jnp.ones(wide(3), BF16)
        kt_ext = jnp.concatenate([kv_all[:, :head_dim], key_bias[:, None, :], ones3, jnp.zeros(wide(LANES - head_dim - 4), BF16)], axis=1)
        vt_ext = jnp.concatenate([kv_all[:, head_dim:], ones3, jnp.zeros(wide(LANES - head_dim - 3), BF16)], axis=1)
        k_ext = kt_ext.transpose(0, 2, 1).reshape(nodes * rows_dev, LANES)
        mixed_t, log_norm = attention_forward(k_ext, vt_ext, qt_ext, heads, head_dim)
        u_bal = dot(mixed_t, w_o, 0, 0).astype(BF16)
        u_part = exchange(u_bal, bal_ix, part_ix, nodes)

        x_wide = x_feat.astype(F32)
        z_mid = (x_wide + jax.nn.relu(pre_act) + x_wide + u_part.astype(F32)).astype(BF16)
        h_pre = dot(z_mid, w_up, 1, 0)
        hidden = jax.nn.gelu(h_pre).astype(BF16)
        keep_row = valid[:, None] > 0
        y_out = jnp.where(keep_row, z_mid.astype(F32) + dot(hidden, w_down, 1, 0), 0.0).astype(BF16)

        g_out = jnp.where(keep_row, y_cot, jnp.zeros_like(y_cot))
        d_hidden = dot(g_out, w_down, 1, 1).astype(BF16)
        gelu_pull = jax.vjp(jax.nn.gelu, h_pre)[1]
        d_hpre = gelu_pull(d_hidden.astype(F32))[0].astype(BF16)
        d_z = (g_out.astype(F32) + dot(d_hpre, w_up, 1, 1)).astype(BF16)
        d_u = exchange(d_z, part_ix, bal_ix, nodes)

        grad_down = dot(hidden, g_out, 0, 0)
        grad_up = dot(z_mid, d_hpre, 0, 0)
        d_pre = jnp.where(pre_act > 0, d_z, jnp.zeros_like(d_z))
        grad_self = dot(x_feat, d_pre, 0, 0)
        grad_msg = dot(agg_msg, d_pre, 0, 0)
        grad_o = dot(mixed_t, d_u, 1, 0)
        grad_msg, grad_self, grad_o, grad_up, grad_down = lax.psum((grad_msg, grad_self, grad_o, grad_up, grad_down), 'nodes')

        do_t = dot(w_o, d_u, 1, 1).astype(BF16)
        delta = jnp.sum((do_t.astype(F32) * mixed_t.astype(F32)).reshape(heads, head_dim, rows_dev), axis=1)
        do_ext = (dot(d_u, pad_heads(w_o, heads, 0), 1, 1) + extra_columns(split3(-delta), heads, head_dim)).astype(BF16)
        col_one = (lax.broadcasted_iota(jnp.int32, (1, heads * LANES), 1) % LANES == head_dim).astype(F32)
        q_ext = (dot(hidden_in, wq_pad, 1, 0) + col_one + extra_columns(split3(-log_norm.reshape(heads, rows_dev)), heads, head_dim + 1)).astype(BF16)
        dkv_t, dq_t = attention_backward(kt_ext, vt_ext, q_ext, do_ext, qt_ext, do_t, heads, head_dim)
        dq_t = (dq_t * scale).astype(BF16)

        d_agg = dot(d_pre, w_msg, 1, 1).astype(BF16)
        d_halo = dot(adj_halo, d_agg, 0, 0).astype(BF16)
        halo_landed = lax.all_to_all(d_halo.reshape(nodes, -1, width), 'nodes', 0, 0, tiled=True).reshape(halo_rows, width)
        local_part = 2.0 * d_z.astype(F32) + dot(d_pre, w_self, 1, 1) + dot(adj_own, d_agg, 0, 0) + dot(halo_pick, halo_landed, 1, 0)

        grad_q = dot(hidden_in, dq_t, 0, 1)
        grad_kv = dot(hidden_in, dkv_t, 0, 1)
        dx_bal = dot(jnp.concatenate([dq_t, dkv_t], axis=0), jnp.concatenate([w_q, w_kv], axis=1), 0, 1).astype(BF16)
        attn_back = exchange(dx_bal, bal_ix, part_ix, nodes)
        dx_feat = (local_part + attn_back.astype(F32)).astype(BF16)
        late = reduce_all(jnp.concatenate([grad_q, grad_kv], axis=1), nodes)
        grad_q, grad_k, grad_v = late[:, :width], late[:, width:width + head_dim], late[:, width + head_dim:]
        return y_out, dx_feat, grad_msg, grad_self, grad_q, grad_k, grad_v, grad_o, grad_up, grad_down

    return jax.shard_map(device_step, mesh=mesh, in_specs=(row_spec, flat_spec, halo_spec, row_spec, row_spec, row_spec, flat_spec, row_spec, row_spec) + (P(),) * 8, out_specs=(row_spec, row_spec) + (grad_spec,) * 8, check_vma=False)
```

time: 1030 us -> 512 us (0.50)
  matrix products: 320 us -> 61.6 us
  Pallas kernels: 0 us -> 235 us
  other arithmetic: 230 us -> 12.6 us
  waiting for transfers between devices: 274 us -> 84.3 us
  local copies, waits for them, and re-layouts: 92.2 us -> 40 us
  blocking collectives: 41.5 us -> 22.9 us
  starting transfers between devices: 47.2 us -> 35.1 us
    dot_general x137 -> x37, matrix products: 320 us -> 61.6 us  [dot(): lax.dot_general(a, b, (((ca,), (cb,)), ((), ())), preferred_element_type=...]
    pallas_call x0 -> x4, Pallas kernels: none -> 235 us  [the longest x1 90.5 us: attention_backward(): pl.pallas_call(functools.partial(backward_kernel, nodes=nodes, heads=head...]
    unnamed x8 -> x1, other arithmetic: 140 us -> 1.79 us
    psum x1, waiting for transfers between devices: 110 us -> 23.4 us  [device_step(): lax.psum((grad_msg, grad_self, grad_o, grad_up, grad_down), 'nodes')]
    reduce_scatter x2 -> x0, waiting for transfers between devices: 85.8 us -> none  [the longest x1 55.7 us: device_step(): lax.psum_scatter(dk_all, 'nodes', scatter_dimension=0, tiled=False)]
    reduce_sum x18 -> x4, other arithmetic: 36.1 us -> 4.6 us  [the longest x1 2.79 us: routes(): part_ix = jnp.sum(jnp.where(hit, code.reshape(-1)[:, None], 0), axis=0)]
    gather x9 -> x0, local copies, waits for them, and re-layouts: 28.3 us -> none  [the longest x4 15.4 us: serve(): picked = jnp.take(source, wanted.reshape(-1), axis=0, mode='clip')]
    scatter-add x3 -> x0, other arithmetic: 20.6 us -> none  [deliver(): jax.ops.segment_sum(flat, wanted.reshape(-1), num_segments=num_rows + 1)]
  transfers between devices with their start and end apart: 13 -> 8, of which waited for: 8 -> 5; matrix products, arithmetic and copies ran while one was open for 36% -> 13% of each run, Pallas kernels for 0% -> 46%
where the time goes in v1:
time: 512 us; the launch traced here: 507 us
  Pallas kernels  235 us (46%)
  waiting for transfers between devices  84.3 us (16%)
  matrix products  61.6 us (12%)
  local copies, waits for them, and re-layouts  40 us (8%)
  starting transfers between devices  35.1 us (7%)
  blocking collectives  22.9 us (4%)
  between operations  15.1 us (3%)
  other arithmetic  12.6 us (2%)
    pallas_call x1, Pallas kernels, attention_backward(): pl.pallas_call(functools.partial(backward_kernel, nodes=nodes, heads=head...  90.5 us
    dot_general x37, matrix products, dot(): lax.dot_general(a, b, (((ca,), (cb,)), ((), ())), preferred_element_type=...  61.6 us
    all_to_all x4, waiting for transfers between devices, exchange(): lax.all_to_all(picked.reshape(nodes, capacity, width), 'nodes', 0, 0, til...  60.8 us
    pallas_call x1, Pallas kernels, reduce_all(): pl.pallas_call(functools.partial(reduce_kernel, nodes=nodes), in_specs=[p...  60.1 us
    pallas_call x1, Pallas kernels, attention_forward(): pl.pallas_call(functools.partial(forward_kernel, blocks=nodes // group, g...  53.3 us
    pallas_call x1, Pallas kernels, build_adjacency(): pl.pallas_call(adjacency_kernel, out_shape=jax.ShapeDtypeStruct((rows, co...  31.3 us
    all_to_all x4, starting transfers between devices, exchange(): lax.all_to_all(picked.reshape(nodes, capacity, width), 'nodes', 0, 0, til...  25.2 us
    unnamed x112, local copies, waits for them, and re-layouts  23.5 us
  transfers between devices with their start and end apart: 8, of which 5 were waited for; matrix products, arithmetic and copies ran while one was open for 13% of the time, Pallas kernels for 46%

profile of v1, /device:TPU:21, one launch (start us, length us, event | category | flops | bytes accessed | tf_op | source)
XLA Modules:
  0.0 506.8 jit_solution(14532048629567484343)
XLA Ops:
  7.2 1.5 convert_reduce_fusion.1
  10.8 22.9 %all-gather.2 = s32[16,1,1152]{2,1,0:T(1,128)S(1)} all-gather(s32[1,1,1152]{2,1,0:T(1,128)S(1)} %reshape.167), channel_id=2, replica_groups=mesh['graphs'=4,'nodes'=16] {'nodes'}, dimensions={0}, use_global_device_ids=true | all-gather | bytes 78336 | tf_op jit(solution)/shard_map/all_gather | solution.py:319
  34.0 2.8 select_reduce_fusion
  36.8 2.6 fusion.18
  39.4 4.4 all-to-all-start.1
  45.5 1.3 convolution_convert_fusion.6
  46.8 18.7 %all-to-all-done.1 = bf16[16,48,512]{2,1,0:T(8,128)(2,1)} async-done(((bf16[16,48,512]{2,1,0:T(8,128)(2,1)}), bf16[16,48,512]{2,1,0:T(8,128)(2,1)}, u32[]{:S(2)}, u32[]{:S(2)}) %all-to-all-start.1) | async-done | bytes 786464 | tf_op jit(solution)/shard_map/all_to_all | solution.py:260
  65.5 4.4 all-to-all-start
  70.5 1.9 fusion.32
  73.4 1.2 fusion.77
  75.8 2.0 copy.56
  77.8 2.1 pad.8
  80.4 1.8 reduce.13
  83.6 2.1 pad.9
  85.8 31.3 %adjacency.1 = bf16[512,1024]{1,0:T(8,128)(2,1)} custom-call(s32[10,2560]{1,0:T(8,128)} %reshape_reshape.3.src_ref, s32[10,2560]{1,0:T(8,128)} %select_n.109.dst_ref), custom_call_target="tpu_custom_call" | custom-call | flops 26843545600 | bytes 1048576 | tf_op jit(solution)/shard_map/adjacency/pallas_call | solution.py:42
  117.1 2.5 fusion.72
  119.6 1.7 add_convert_fusion.2.q_ref.qt_ref
  121.4 1.8 fusion.146
  123.2 3.1 maximum_maximum_fusion
  126.2 3.9 copy.55
  130.1 53.3 %attention_forward.1 = (bf16[512,512]{1,0:T(8,128)(2,1)}, f32[8,1,512]{2,1,0:T(1,128)}) custom-call(bf16[8192,128]{1,0:T(8,128)(2,1)} %bitcast.97, bf16[16,128,512]{2,1,0:T(8,128)(2,1)} %get-tuple-element.75.vt_ref, bf16[1024,512]{1,0:T(8,128)(2,1)} %add_convert_fusion.2.q_ref.qt_ref), custom_call_target="tpu_custom_call" | custom-call | flops 8589934592 | bytes 8388608 | tf_op jit(solution)/shard_map/attention_forward/pallas_call | solution.py:82
  183.4 2.9 fusion.20
  186.3 7.6 %all-to-all-start.2 = ((bf16[16,48,512]{2,1,0:T(8,128)(2,1)}), bf16[16,48,512]{2,1,0:T(8,128)(2,1)}, u32[]{:S(2)}, u32[]{:S(2)}) async-start(bf16[16,48,512]{2,1,0:T(8,128)(2,1)} %bitcast.10), calls=%async_computation.2 | async-start | bytes 1572864 | tf_op jit(solution)/shard_map/all_to_all | solution.py:260
  194.0 2.1 fusion.38
  196.6 1.4 convolution_add_fusion.3
  198.8 1.5 add_convert_fusion.1.q_ref
  200.3 15.1 %all-to-all-done.2 = bf16[16,48,512]{2,1,0:T(8,128)(2,1)} async-done(((bf16[16,48,512]{2,1,0:T(8,128)(2,1)}), bf16[16,48,512]{2,1,0:T(8,128)(2,1)}, u32[]{:S(2)}, u32[]{:S(2)}) %all-to-all-start.2) | async-done | bytes 786464 | tf_op jit(solution)/shard_map/all_to_all | solution.py:260
  215.4 2.1 fusion.36
  217.5 1.3 fusion.149
  219.4 3.6 fusion.2
  223.0 1.3 compare_select_fusion
  224.4 1.5 fusion.19
  226.3 1.5 fusion.152
  227.8 1.4 convolution_bitcast_fusion
  229.2 4.6 all-to-all-start.4
  235.4 1.4 convolution_add_fusion.1
  236.9 3.3 fusion.156
  240.2 3.8 fusion.144
  244.0 11.7 %all-to-all-done.4 = bf16[16,48,512]{2,1,0:T(8,128)(2,1)} async-done(((bf16[16,48,512]{2,1,0:T(8,128)(2,1)}), bf16[16,48,512]{2,1,0:T(8,128)(2,1)}, u32[]{:S(2)}, u32[]{:S(2)}) %all-to-all-start.4) | async-done | bytes 786464 | tf_op jit(solution)/shard_map/all_to_all | solution.py:260
  255.7 1.8 fusion.29
  257.5 1.3 bitcast_reduce_fusion
  258.8 1.4 fusion.155
  261.5 1.5 copy-done.2
  263.1 1.6 copy-done.3
  264.7 1.2 copy-done.4
  265.9 1.0 copy-done.5
  266.9 1.2 copy-done.6
  268.1 90.5 %attention_backward.1 = (bf16[128,512]{1,0:T(8,128)(2,1)S(1)}, f32[512,512]{1,0:T(8,128)S(1)}) custom-call(bf16[16,128,512]{2,1,0:T(8,128)(2,1)S(1)} %copy-done.2, bf16[16,128,512]{2,1,0:T(8,128)(2,1)S(1)} %copy-done.3, bf16[512,1024]{1,0:T(8,128)(2,1)S(1)} %copy-done.4, bf16[512,1024]{1,0:T(8,128)(2,1)S(1)} %add_convert_fusion.do_ref, ...), custom_call_target="tpu_custom_call" | custom-call | flops 21474836480 | bytes 16777216 | tf_op jit(solution)/shard_map/attention_backward/pallas_call | solution.py:161
  358.8 3.3 fusion.21
  362.1 8.6 %all-to-all-start.5 = ((bf16[16,48,512]{2,1,0:T(8,128)(2,1)}), bf16[16,48,512]{2,1,0:T(8,128)(2,1)}, u32[]{:S(2)}, u32[]{:S(2)}) async-start(bf16[16,48,512]{2,1,0:T(8,128)(2,1)} %bitcast.101), calls=%async_computation.5 | async-start | bytes 1572864 | tf_op jit(solution)/shard_map/all_to_all | solution.py:260
  370.7 1.3 convolution_convert_fusion.3
  371.9 5.2 %fusion.24 = bf16[512,512]{1,0:T(8,128)(2,1)} fusion(bf16[2048,512]{1,0:T(8,128)(2,1)} %param.33, bf16[512,512]{1,0:T(8,128)(2,1)S(1)} %copy-done.33, pred[512]{0:T(512)(128)(4,1)S(1)} %get-tuple-element.66, f32[512,2048]{1,0:T(8,128)} %copy-done.19), kind=kOutput, calls=%fused_computation.48 | convolution fusion | flops 1084227584 | bytes 7340544 | tf_op jit(solution)/shard_map/dot_general | solution.py:17
  378.1 15.2 %all-to-all-done.5 = bf16[16,48,512]{2,1,0:T(8,128)(2,1)} async-done(((bf16[16,48,512]{2,1,0:T(8,128)(2,1)}), bf16[16,48,512]{2,1,0:T(8,128)(2,1)}, u32[]{:S(2)}, u32[]{:S(2)}) %all-to-all-start.5) | async-done | bytes 786464 | tf_op jit(solution)/shard_map/all_to_all | solution.py:260
  393.3 4.6 all-to-all-start.3
  397.9 60.1 %reduce_all.1 = f32[512,640]{1,0:T(8,128)S(1)} custom-call(f32[512,640]{1,0:T(8,128)S(1)} %pad_maximum_fusion.x_ref), custom_call_target="tpu_custom_call" | custom-call | flops 10000000000 | bytes 8388608 | tf_op jit(solution)/shard_map/reduce_all/pallas_call | solution.py:240
  458.1 1.1 slice.37
  460.9 1.8 fusion.33
  462.6 1.2 fusion.25
  463.9 23.4 %all-reduce.5.cloned.1.call-done = (f32[512,512]{1,0:T(8,128)}, f32[512,512]{0,1:T(8,128)}, f32[512,512]{1,0:T(8,128)}, f32[512,2048]{1,0:T(8,128)}, f32[2048,512]{1,0:T(8,128)}) async-done(((f32[512,512]{1,0:T(8,128)}, f32[512,512]{0,1:T(8,128)}, f32[512,512]{1,0:T(8,128)}, f32[512,2048]{1,0:T(8,128)}, f32[2048,512]{1,0:T(8,128)}), (f32[512,512]{1,0:T(8,128)}, f32[512,512]{0,1:T(8,128)}, ...) | async-done | bytes 11534352 | tf_op jit(solution)/shard_map/psum | solution.py:376
  487.3 2.7 copy.61
  491.9 1.0 copy-done.17
  492.9 2.1 copy.85
  495.0 1.6 copy-done.16
  496.6 2.1 copy.86
  (156 shorter events, 19.4 us)
Async XLA Ops:
  7.2 210.3 %copy-start = (bf16[512,2048]{1,0:T(8,128)(2,1)S(1)}, bf16[512,2048]{1,0:T(8,128)(2,1)}, u32[]{:S(2)}) copy-start(bf16[512,2048]{1,0:T(8,128)(2,1)} %param.32) | copy-start | bytes 6291460
  34.0 10.4 %copy-start.44 = (s32[512]{0:T(512)S(1)}, s32[512]{0:T(512)}, u32[]{:S(2)}) copy-start(s32[512]{0:T(512)} %param.23) | copy-start | bytes 6148
  36.8 7.8 %copy-start.39 = (bf16[512,512]{1,0:T(8,128)(2,1)S(1)}, bf16[512,512]{1,0:T(8,128)(2,1)}, u32[]{:S(2)}) copy-start(bf16[512,512]{1,0:T(8,128)(2,1)} %param.28) | copy-start | bytes 1572868
  36.8 8.7 %copy-start.9 = (bf16[512,512]{1,0:T(8,128)(2,1)S(1)}, bf16[512,512]{1,0:T(8,128)(2,1)}, u32[]{:S(2)}) copy-start(bf16[512,512]{1,0:T(8,128)(2,1)} %param.17) | copy-start | bytes 1572868
  39.4 26.1 %all-to-all-start.1 = ((bf16[16,48,512]{2,1,0:T(8,128)(2,1)}), bf16[16,48,512]{2,1,0:T(8,128)(2,1)}, u32[]{:S(2)}, u32[]{:S(2)}) async-start(bf16[16,48,512]{2,1,0:T(8,128)(2,1)} %bitcast.100), calls=%async_computation.1 | async-start | bytes 1572864 | tf_op jit(solution)/shard_map/all_to_all | solution.py:260
  46.8 25.6 %copy-start.41 = (bf16[512,64]{0,1:T(8,128)(2,1)S(1)}, bf16[512,64]{0,1:T(8,128)(2,1)}, u32[]{:S(2)}) copy-start(bf16[512,64]{0,1:T(8,128)(2,1)} %param.30) | copy-start | bytes 196612
  46.8 25.6 %copy-start.42 = (bf16[512,64]{0,1:T(8,128)(2,1)S(1)}, bf16[512,64]{0,1:T(8,128)(2,1)}, u32[]{:S(2)}) copy-start(bf16[512,64]{0,1:T(8,128)(2,1)} %param.29) | copy-start | bytes 196612
  65.5 120.8 %all-to-all-start = ((bf16[16,32,512]{2,1,0:T(8,128)(2,1)}), bf16[16,32,512]{2,1,0:T(8,128)(2,1)}, u32[]{:S(2)}, u32[]{:S(2)}) async-start(bf16[16,32,512]{2,1,0:T(8,128)(2,1)} %bitcast), calls=%async_computation | async-start | bytes 1048576 | tf_op jit(solution)/shard_map/all_to_all | solution.py:340
  69.9 3.6 copy-start.43
  69.9 51.5 %all-gather.5.cloned.1.call-start = ((), (), s32[]{:S(2)}) async-start(), calls=%async_computation.6 | async-start | bytes 2228224 | tf_op jit(solution)/shard_map/all_gather | solution.py:332
  72.4 125.6 %copy-start.7 = (bf16[512,512]{1,0:T(8,128)(2,1)}, bf16[512,512]{1,0:T(8,128)(2,1)S(1)}, u32[]{:S(2)}) copy-start(bf16[512,512]{1,0:T(8,128)(2,1)S(1)} %fusion.32) | copy-start | bytes 1572868
  117.1 2.5 copy-start.14
  130.1 53.3 %copy-start.37 = (bf16[512,512]{1,0:T(8,128)(2,1)S(1)}, bf16[512,512]{1,0:T(8,128)(2,1)}, u32[]{:S(2)}) copy-start(bf16[512,512]{1,0:T(8,128)(2,1)} %param.31) | copy-start | bytes 1572868
  186.3 29.1 %all-to-all-start.2 = ((bf16[16,48,512]{2,1,0:T(8,128)(2,1)}), bf16[16,48,512]{2,1,0:T(8,128)(2,1)}, u32[]{:S(2)}, u32[]{:S(2)}) async-start(bf16[16,48,512]{2,1,0:T(8,128)(2,1)} %bitcast.10), calls=%async_computation.2 | async-start | bytes 1572864 | tf_op jit(solution)/shard_map/all_to_all | solution.py:260
  193.9 2.1 copy-start.27
  194.0 2.6 copy-start.10
  194.0 2.6 copy-start.25
  196.5 1.4 copy-start.15
  198.0 0.8 copy-start.45
  198.7 16.7 %copy-start.11 = (bf16[512,512]{1,0:T(8,128)(2,1)S(1)}, bf16[512,512]{1,0:T(8,128)(2,1)}, u32[]{:S(2)}) copy-start(bf16[512,512]{1,0:T(8,128)(2,1)} %param.17) | copy-start | bytes 1572868
  217.5 1.3 copy-start.31
  217.5 1.8 copy-start.46
  217.5 1.9 copy-start.47
  218.9 4.1 copy-start.19
  219.4 3.6 copy-start.34
  223.0 1.3 copy-start.23
  224.4 1.5 copy-start.26
  225.9 1.9 copy-start.12
  227.8 6.3 %copy-start.28 = (bf16[512,512]{1,0:T(8,128)(2,1)S(1)}, bf16[512,512]{1,0:T(8,128)(2,1)}, u32[]{:S(2)}) copy-start(bf16[512,512]{1,0:T(8,128)(2,1)} %param.26) | copy-start | bytes 1572868
  229.2 6.2 %copy-start.21 = (bf16[512,1024]{1,0:T(8,128)(2,1)S(1)}, bf16[512,1024]{1,0:T(8,128)(2,1)}, u32[]{:S(2)}) copy-start(bf16[512,1024]{1,0:T(8,128)(2,1)} %adjacency.1) | copy-start | bytes 3145732
  229.2 26.5 %all-to-all-start.4 = ((bf16[16,48,512]{2,1,0:T(8,128)(2,1)}), bf16[16,48,512]{2,1,0:T(8,128)(2,1)}, u32[]{:S(2)}, u32[]{:S(2)}) async-start(bf16[16,48,512]{2,1,0:T(8,128)(2,1)} %bitcast.102), calls=%async_computation.4 | async-start | bytes 1572864 | tf_op jit(solution)/shard_map/all_to_all | solution.py:260
  233.8 253.4 %all-reduce.5.cloned.1.call-start = ((), (), s32[]{:S(2)}) async-start(), calls=%async_computation.7 | async-start | bytes 23068672 | tf_op jit(solution)/shard_map/psum | solution.py:376
  234.1 2.7 copy-start.24
  234.1 2.7 copy-start.32
  234.6 0.8 copy-start.29
  236.9 3.3 copy-start.20
  236.9 3.3 copy-start.48
  244.0 13.4 %copy-start.38 = (bf16[512,512]{1,0:T(8,128)(2,1)S(1)}, bf16[512,512]{1,0:T(8,128)(2,1)}, u32[]{:S(2)}) copy-start(bf16[512,512]{1,0:T(8,128)(2,1)} %param.31) | copy-start | bytes 1572868
  244.0 13.5 %copy-start.40 = (bf16[512,512]{1,0:T(8,128)(2,1)S(1)}, bf16[512,512]{1,0:T(8,128)(2,1)}, u32[]{:S(2)}) copy-start(bf16[512,512]{1,0:T(8,128)(2,1)} %get-tuple-element.14) | copy-start | bytes 1572868
  257.5 2.7 copy-start.13
  261.5 1.6 copy-start.2
  263.1 1.6 copy-start.3
  264.7 1.2 copy-start.4
  265.9 1.0 copy-start.5
  266.9 1.2 copy-start.6
  358.8 11.9 %copy-start.22 = (bf16[512,1024]{1,0:T(8,128)(2,1)S(1)}, bf16[512,1024]{1,0:T(8,128)(2,1)}, u32[]{:S(2)}) copy-start(bf16[512,1024]{1,0:T(8,128)(2,1)} %adjacency.1) | copy-start | bytes 3145732
  358.8 11.9 %copy-start.30 = (bf16[512,512]{1,0:T(8,128)(2,1)S(1)}, bf16[512,512]{1,0:T(8,128)(2,1)}, u32[]{:S(2)}) copy-start(bf16[512,512]{1,0:T(8,128)(2,1)} %copy-done.29) | copy-start | bytes 1572868
  362.1 9.9 %copy-start.33 = (bf16[512,512]{1,0:T(8,128)(2,1)S(1)}, bf16[512,512]{1,0:T(8,128)(2,1)}, u32[]{:S(2)}) copy-start(bf16[512,512]{1,0:T(8,128)(2,1)} %copy-done.31) | copy-start | bytes 1572868
  362.1 31.3 %all-to-all-start.5 = ((bf16[16,48,512]{2,1,0:T(8,128)(2,1)}), bf16[16,48,512]{2,1,0:T(8,128)(2,1)}, u32[]{:S(2)}, u32[]{:S(2)}) async-start(bf16[16,48,512]{2,1,0:T(8,128)(2,1)} %bitcast.101), calls=%async_computation.5 | async-start | bytes 1572864 | tf_op jit(solution)/shard_map/all_to_all | solution.py:260
  371.9 5.2 %copy-start.8 = (bf16[512,512]{1,0:T(8,128)(2,1)S(1)}, bf16[512,512]{1,0:T(8,128)(2,1)}, u32[]{:S(2)}) copy-start(bf16[512,512]{1,0:T(8,128)(2,1)} %copy-done.7) | copy-start | bytes 1572868
  393.3 69.3 %all-to-all-start.3 = ((bf16[16,32,512]{2,1,0:T(8,128)(2,1)}), bf16[16,32,512]{2,1,0:T(8,128)(2,1)S(1)}, u32[]{:S(2)}, u32[]{:S(2)}) async-start(bf16[16,32,512]{2,1,0:T(8,128)(2,1)} %bitcast.12), calls=%async_computation.3 | async-start | bytes 1048576 | tf_op jit(solution)/shard_map/all_to_all | solution.py:388
  459.2 3.5 copy-start.18
  487.3 2.7 copy-start.36
  487.3 3.7 copy-start.35
  489.9 2.9 copy-start.17
  492.9 3.7 copy-start.16
  496.6 3.1 copy-start.1
Sparse Core Ops, SparseCore 0:
  73.6 37.6 all-gather.4
  261.7 225.5 all-reduce.4

commit v2 on v1

--- a/solution.py
+++ b/solution.py
@@ -17,85 +17,270 @@
     return lax.dot_general(a, b, (((ca,), (cb,)), ((), ())), preferred_element_type=F32)
 
 
-def adjacency_kernel(src_ref, dst_ref, out_ref, acc_ref):
-    rows, cols = out_ref.shape
+def entry_kernel(x_ref, info_ref, halo_ref, src_ref, dst_ref, x_bal_ref, adj_ref, bal_ix_ref, part_ix_ref, info_all, halo_got, acc_ref, own_ref, rank_ref, send_buf, recv_buf, info_send, info_recv, halo_send, halo_recv, row_send, row_recv, *, nodes):
+    me = lax.axis_index('nodes')
+    rows = x_ref.shape[0]
+    cols = adj_ref.shape[1]
     steps, chunk = src_ref.shape
+    capacity = send_buf.shape[1]
+    peer = lambda k: lax.rem(me + k, nodes)
+    barrier = pltpu.get_barrier_semaphore()
+
+    def greet(k, c):
+        pl.semaphore_signal(barrier, inc=1, device_id={'nodes': peer(k)}, device_id_type=MESH)
+        return c
+
+    lax.fori_loop(1, nodes, greet, 0)
     acc_ref[...] = jnp.zeros_like(acc_ref)
     dst_iota = lax.broadcasted_iota(jnp.int32, (rows, chunk), 0)
     src_iota = lax.broadcasted_iota(jnp.int32, (cols, chunk), 0)
 
-    def body(i, c):
+    def count(i, c):
         left = jnp.where(dst_iota == dst_ref[pl.ds(i, 1), :], 1.0, 0.0).astype(BF16)
         right = jnp.where(src_iota == src_ref[pl.ds(i, 1), :], 1.0, 0.0).astype(BF16)
         acc_ref[...] += dot(left, right, 1, 1)
         return c
 
-    lax.fori_loop(0, steps, body, 0)
-    out_ref[...] = acc_ref[...].astype(BF16)
-
-
-def build_adjacency(edge_src, edge_dst, rows, cols, chunk=2560):
+    first, second = steps // 10, steps // 2
+    lax.fori_loop(0, first, count, 0)
+    pl.semaphore_wait(barrier, nodes - 1)
+
+    def tell(k):
+        return pltpu.make_async_remote_copy(src_ref=info_ref.at[0], dst_ref=info_all.at[me], send_sem=info_send.at[k], recv_sem=info_recv.at[k], device_id={'nodes': peer(k)}, device_id_type=MESH)
+
+    def ask(k):
+        return pltpu.make_async_remote_copy(src_ref=halo_ref.at[peer(k)], dst_ref=halo_got.at[me], send_sem=halo_send.at[k], recv_sem=halo_recv.at[k], device_id={'nodes': peer(k)}, device_id_type=MESH)
+
+    def give(k):
+        return pltpu.make_async_remote_copy(src_ref=send_buf.at[k], dst_ref=recv_buf.at[me], send_sem=row_send.at[k], recv_sem=row_recv.at[k], device_id={'nodes': peer(k)}, device_id_type=MESH)
+
+    def start_info(k, c):
+        tell(k).start()
+        ask(k).start()
+        return c
+
+    lax.fori_loop(1, nodes, start_info, 0)
+    info_all[me] = info_ref[0]
+    halo_got[me] = halo_ref[me]
+    lax.fori_loop(first, second, count, 0)
+
+    def wait_info(k, c):
+        tell(k).wait_recv()
+        return c
+
+    lax.fori_loop(1, nodes, wait_info, 0)
+
+    def mark(q, c):
+        own_ref[pl.ds(q, 1), :] = jnp.where(lax.div(info_all[q][:, :rows], rows) == me, 1.0, 0.0)
+        return c
+
+    lax.fori_loop(0, nodes, mark, 0)
+    before = jnp.where(lax.broadcasted_iota(jnp.int32, (rows, rows), 0) < lax.broadcasted_iota(jnp.int32, (rows, rows), 1), 1.0, 0.0).astype(BF16)
+    rank_ref[...] = dot(own_ref[...].astype(BF16), before, 1, 0)
+    slot_iota = lax.broadcasted_iota(jnp.int32, (rows, rows), 0)
+    cap_iota = lax.broadcasted_iota(jnp.int32, (capacity, rows), 0)
+    x = x_ref[...]
+
+    def pick_rows(k, part_ix):
+        q = peer(k)
+        perm = info_all[q][:, :rows]
+        own = lax.div(perm, rows) == me
+        rank = jnp.where(own, rank_ref[pl.ds(q, 1), :].astype(jnp.int32), -1)
+        ranked = jnp.where(cap_iota == rank, 1.0, 0.0).astype(BF16)
+        placed = jnp.where(slot_iota == lax.rem(perm, rows), 1.0, 0.0).astype(BF16)
+        pick = dot(ranked, placed, 1, 1)
+        send_buf[k] = dot(pick.astype(BF16), x, 1, 0).astype(BF16)
+
+        @pl.when(k > 0)
+        def _():
+            give(k).start()
+
+        code = (cap_iota + q * capacity).astype(F32)
+        return part_ix + jnp.sum(pick * code, axis=0, keepdims=True)
+
+    part_ix = lax.fori_loop(0, nodes, pick_rows, jnp.zeros((1, rows), F32))
+    part_ix_ref[...] = part_ix.astype(jnp.int32)
+    recv_buf[me] = send_buf[0]
+    lax.fori_loop(second, steps, count, 0)
+    adj_ref[...] = acc_ref[...].astype(BF16)
+
+    owner = lax.div(info_ref[0][:, :rows], rows)
+    owners = lax.broadcasted_iota(jnp.int32, (nodes, rows), 0) == owner
+    ranks = dot(jnp.where(owners, 1.0, 0.0).astype(BF16), before, 1, 0)
+    bal_ix = owner * capacity + jnp.sum(jnp.where(owners, ranks, 0.0), axis=0, keepdims=True).astype(jnp.int32)
+    bal_ix_ref[...] = bal_ix
+
+    def wait_rows(k, c):
+        give(k).wait_recv()
+        ask(k).wait_recv()
+        return c
+
+    lax.fori_loop(1, nodes, wait_rows, 0)
+    landed = jnp.where(lax.broadcasted_iota(jnp.int32, (nodes * capacity, rows), 0) == bal_ix, 1.0, 0.0).astype(BF16)
+    x_bal_ref[...] = dot(landed, recv_buf[...].reshape(nodes * capacity, x.shape[1]), 0, 0).astype(BF16)
+
+    def wait_sends(k, c):
+        tell(k).wait_send()
+        ask(k).wait_send()
+        give(k).wait_send()
+        return c
+
+    lax.fori_loop(1, nodes, wait_sends, 0)
+
+
+def entry(x, info, halo, edge_src, edge_dst, nodes, chunk=2560):
+    rows, width = x.shape
     edges = edge_src.size
     if edges % chunk:
         chunk = LANES
     steps = edges // chunk
+    capacity = rows // nodes + rows // (2 * nodes)
+    cols = 2 * rows
+    i32 = jnp.int32
+    sems = lambda: pltpu.SemaphoreType.DMA((nodes,))
     return pl.pallas_call(
-        adjacency_kernel,
-        out_shape=jax.ShapeDtypeStruct((rows, cols), BF16),
-        scratch_shapes=[pltpu.VMEM((rows, cols), F32)],
-        cost_estimate=pl.CostEstimate(flops=2 * edges * rows * cols, bytes_accessed=2 * rows * cols, transcendentals=0),
-        name='adjacency',
-    )(edge_src.reshape(steps, chunk), edge_dst.reshape(steps, chunk))
-
-
-def forward_kernel(k_ref, vt_ref, q_ref, o_ref, lse_ref, *, blocks, group, unroll):
+        functools.partial(entry_kernel, nodes=nodes),
+        in_specs=[pl.BlockSpec(memory_space=pltpu.VMEM)] * 5,
+        out_specs=[pl.BlockSpec(memory_space=pltpu.VMEM)] * 6,
+        out_shape=[
+            jax.ShapeDtypeStruct((rows, width), BF16),
+            jax.ShapeDtypeStruct((rows, cols), BF16),
+            jax.ShapeDtypeStruct((1, rows), i32),
+            jax.ShapeDtypeStruct((1, rows), i32),
+            jax.ShapeDtypeStruct((nodes,) + info.shape[1:], i32),
+            jax.ShapeDtypeStruct(halo.shape, i32),
+        ],
+        scratch_shapes=[
+            pltpu.VMEM((rows, cols), F32),
+            pltpu.VMEM((nodes, rows), F32),
+            pltpu.VMEM((nodes, rows), F32),
+            pltpu.VMEM((nodes, capacity, width), BF16),
+            pltpu.VMEM((nodes, capacity, width), BF16),
+            sems(), sems(), sems(), sems(), sems(), sems(),
+        ],
+        compiler_params=pltpu.CompilerParams(vmem_limit_bytes=40 * 2**20, collective_id=2, has_side_effects=True),
+        cost_estimate=pl.CostEstimate(flops=2 * edges * rows * cols, bytes_accessed=2**22, transcendentals=0),
+        name='entry',
+    )(x, info, halo, edge_src.reshape(steps, chunk), edge_dst.reshape(steps, chunk))
+
+
+def forward_kernel(kv_ref, bias_ref, q_ref, o_ref, lse_ref, kt_ref, vt_ref, kv_all, k_pair, max_ref, sum_ref, acc_ref, to_right, from_left, to_left, from_right, *, nodes, heads, head_dim, unroll):
+    me = lax.axis_index('nodes')
+    part = kv_ref.shape[1]
     rows = q_ref.shape[1]
-    head_dim = o_ref.shape[0]
-    part = vt_ref.shape[2]
-    bk = part * group
-    q = q_ref[...]
-
-    def body(j, carry):
-        run_max, run_sum, acc = carry
-        start = pl.multiple_of(j * bk, bk)
-        scores = dot(k_ref[pl.ds(start, bk), :], q, 1, 0)
-        new_max = jnp.maximum(run_max, jnp.max(scores, axis=0, keepdims=True))
-        prob = jnp.exp(scores - new_max)
-        decay = jnp.exp(run_max - new_max)
-        run_sum = run_sum * decay + jnp.sum(prob, axis=0, keepdims=True)
-        prob = prob.astype(BF16)
-        acc = acc * decay
-        for g in range(group):
-            acc = acc + dot(vt_ref[j * group + g, :head_dim, :], prob[g * part:(g + 1) * part], 1, 0)
-        return new_max, run_sum, acc
-
-    init = (jnp.full((1, rows), -jnp.inf, F32), jnp.zeros((1, rows), F32), jnp.zeros((head_dim, rows), F32))
-    run_max, run_sum, acc = lax.fori_loop(0, blocks, body, init, unroll=unroll)
-    o_ref[...] = (acc / run_sum).astype(BF16)
-    lse_ref[0] = run_max + jnp.log(run_sum)
-
-
-def attention_forward(k_ext, vt_ext, qt_ext, heads, head_dim, group=4, unroll=2):
-    keys = k_ext.shape[0]
+    half = nodes // 2
+    right, left = lax.rem(me + 1, nodes), lax.rem(me + nodes - 1, nodes)
+    barrier = pltpu.get_barrier_semaphore()
+    for neighbour in (left, right):
+        pl.semaphore_signal(barrier, inc=1, device_id={'nodes': neighbour}, device_id_type=MESH)
+    pl.semaphore_wait(barrier, 2)
+
+    def hop(src, j, t, send, recv, to):
+        return pltpu.make_async_remote_copy(src_ref=src, dst_ref=kv_all.at[j], send_sem=send.at[t], recv_sem=recv.at[t], device_id={'nodes': to}, device_id_type=MESH)
+
+    hop(kv_ref, me, 0, to_left, from_right, left).start()
+    hop(kv_ref, me, 0, to_right, from_left, right).start()
+    kv_all[me] = kv_ref[...]
+    max_ref[...] = jnp.full(max_ref.shape, -jnp.inf, F32)
+    sum_ref[...] = jnp.zeros_like(sum_ref)
+    acc_ref[...] = jnp.zeros_like(acc_ref)
+    row_iota = lax.broadcasted_iota(jnp.int32, (head_dim, part), 0)
+    v_extra = jnp.where(row_iota < 3, 1.0, 0.0).astype(BF16)
+
+    def widen(j, g):
+        block = kv_all[j]
+        k_extra = jnp.where(row_iota == 0, bias_ref[j], jnp.where(row_iota < 4, 1.0, 0.0)).astype(BF16)
+        wide = jnp.concatenate([block[:head_dim], k_extra], axis=0)
+        kt_ref[j] = wide
+        vt_ref[j, :head_dim, :] = block[head_dim:]
+        vt_ref[j, head_dim:, :] = v_extra
+        k_pair[g * part:(g + 1) * part, :] = wide.T
+
+    def step(t, c):
+        jr = lax.rem(me + 1 + t, nodes)
+        jl = lax.rem(me + nodes - t, nodes)
+        hop(kv_all.at[jr], jr, t, to_left, from_right, left).wait_recv()
+
+        @pl.when(t < half - 1)
+        def _():
+            hop(kv_all.at[jr], jr, t + 1, to_left, from_right, left).start()
+
+        @pl.when(t > 0)
+        def _():
+            hop(kv_all.at[jl], jl, t - 1, to_right, from_left, right).wait_recv()
+
+        @pl.when((t > 0) & (t < half - 1))
+        def _():
+            hop(kv_all.at[jl], jl, t, to_right, from_left, right).start()
+
+        widen(jl, 0)
+        widen(jr, 1)
+        vl = kv_all[jl, head_dim:, :]
+        vr = kv_all[jr, head_dim:, :]
+
+        def body(h, c):
+            lo = pl.multiple_of(h * LANES, LANES)
+            r0 = pl.multiple_of(h * head_dim, head_dim)
+            scores = dot(k_pair[...], q_ref[pl.ds(lo, LANES), :], 1, 0)
+            old_max = max_ref[h]
+            new_max = jnp.maximum(old_max, jnp.max(scores, axis=0, keepdims=True))
+            prob = jnp.exp(scores - new_max)
+            decay = jnp.exp(old_max - new_max)
+            max_ref[h] = new_max
+            sum_ref[h] = sum_ref[h] * decay + jnp.sum(prob, axis=0, keepdims=True)
+            prob = prob.astype(BF16)
+            acc_ref[pl.ds(r0, head_dim), :] = acc_ref[pl.ds(r0, head_dim), :] * decay + (dot(vl, prob[:part], 1, 0) + dot(vr, prob[part:], 1, 0))
+            return c
+
+        return lax.fori_loop(0, heads, body, c, unroll=unroll)
+
+    lax.fori_loop(0, half, step, 0)
+
+    def finish(h, c):
+        r0 = pl.multiple_of(h * head_dim, head_dim)
+        o_ref[pl.ds(r0, head_dim), :] = (acc_ref[pl.ds(r0, head_dim), :] / sum_ref[h]).astype(BF16)
+        lse_ref[h] = max_ref[h] + jnp.log(sum_ref[h])
+        return c
+
+    lax.fori_loop(0, heads, finish, 0)
+
+    def drain(t, c):
+        hop(kv_ref, me, t, to_left, from_right, left).wait_send()
+
+        @pl.when(t < half - 1)
+        def _():
+            hop(kv_ref, me, t, to_right, from_left, right).wait_send()
+        return c
+
+    lax.fori_loop(0, half, drain, 0)
+
+
+def attention_forward(kv_t, key_bias, qt_ext, nodes, heads, head_dim, unroll=4):
+    part = kv_t.shape[1]
     rows = qt_ext.shape[1]
-    nodes, wide, part = vt_ext.shape
+    half = nodes // 2
+    wide = jax.ShapeDtypeStruct((nodes, LANES, part), BF16)
+    sems = lambda: pltpu.SemaphoreType.DMA((half,))
     return pl.pallas_call(
-        functools.partial(forward_kernel, blocks=nodes // group, group=group, unroll=unroll),
-        grid=(heads,),
-        in_specs=[
-            pl.BlockSpec((keys, LANES), lambda h: (0, 0)),
-            pl.BlockSpec((nodes, wide, part), lambda h: (0, 0, 0)),
-            pl.BlockSpec((LANES, rows), lambda h: (h, 0)),
+        functools.partial(forward_kernel, nodes=nodes, heads=heads, head_dim=head_dim, unroll=unroll),
+        in_specs=[pl.BlockSpec(memory_space=pltpu.VMEM)] * 3,
+        out_specs=[pl.BlockSpec(memory_space=pltpu.VMEM)] * 4,
+        out_shape=[jax.ShapeDtypeStruct((heads * head_dim, rows), BF16), jax.ShapeDtypeStruct((heads, 1, rows), F32), wide, wide],
+        scratch_shapes=[
+            pltpu.VMEM((nodes, 2 * head_dim, part), BF16),
+            pltpu.VMEM((2 * part, LANES), BF16),
+            pltpu.VMEM((heads, 1, rows), F32),
+            pltpu.VMEM((heads, 1, rows), F32),
+            pltpu.VMEM((heads * head_dim, rows), F32),
+            sems(), sems(), sems(), sems(),
         ],
-        out_specs=[pl.BlockSpec((head_dim, rows), lambda h: (h, 0)), pl.BlockSpec((1, 1, rows), lambda h: (h, 0, 0))],
-        out_shape=[jax.ShapeDtypeStruct((heads * head_dim, rows), BF16), jax.ShapeDtypeStruct((heads, 1, rows), F32)],
-        compiler_params=pltpu.CompilerParams(vmem_limit_bytes=56 * 2**20),
-        cost_estimate=pl.CostEstimate(flops=4 * heads * rows * keys * head_dim, bytes_accessed=2**23, transcendentals=heads * rows * keys),
+        compiler_params=pltpu.CompilerParams(vmem_limit_bytes=40 * 2**20, collective_id=3, has_side_effects=True),
+        cost_estimate=pl.CostEstimate(flops=4 * heads * rows * nodes * part * head_dim, bytes_accessed=2**23, transcendentals=heads * rows * nodes * part),
         name='attention_forward',
-    )(k_ext, vt_ext, qt_ext)
-
-
-def backward_kernel(kt_ref, vt_ref, q_ref, do_ref, qt_ref, dot_ref, dkv_ref, dq_ref, sums, send_sem, recv_sem, *, nodes, heads, head_dim, unroll):
+    )(kv_t, key_bias, qt_ext)
+
+
+def backward_kernel(kt_ref, vt_ref, q_ref, do_ref, qt_ref, dot_ref, dkv_ref, dq_ref, sums_r, sums_l, send_r, recv_r, send_l, recv_l, *, nodes, heads, head_dim, unroll):
     bk = kt_ref.shape[-1]
     me = lax.axis_index('nodes')
     right, left = lax.rem(me + 1, nodes), lax.rem(me + nodes - 1, nodes)
@@ -105,13 +290,18 @@
     pl.semaphore_wait(barrier, 2)
     dq_ref[...] = jnp.zeros_like(dq_ref)
 
-    def hop(t):
-        return pltpu.make_async_remote_copy(src_ref=sums.at[t], dst_ref=sums.at[t + 1], send_sem=send_sem.at[t], recv_sem=recv_sem.at[t + 1], device_id={'nodes': right}, device_id_type=MESH)
+    half = bk // 2
+    rings = ((sums_r, send_r, recv_r, right, slice(0, half)), (sums_l, send_l, recv_l, left, slice(half, bk)))
+
+    def hop(ring, t):
+        sums, send_sem, recv_sem, to, cols = ring
+        return pltpu.make_async_remote_copy(src_ref=sums.at[t], dst_ref=sums.at[t + 1], send_sem=send_sem.at[t], recv_sem=recv_sem.at[t + 1], device_id={'nodes': to}, device_id_type=MESH)
 
     def step(t, c):
-        j = lax.rem(me + 2 * nodes - 1 - t, nodes)
-        kt = kt_ref[j]
-        vt = vt_ref[j]
+        jr = lax.rem(me + 2 * nodes - 1 - t, nodes)
+        jl = lax.rem(me + 1 + t, nodes)
+        kt = jnp.concatenate([kt_ref[jr, :, :half], kt_ref[jl, :, half:]], axis=1)
+        vt = jnp.concatenate([vt_ref[jr, :, :half], vt_ref[jl, :, half:]], axis=1)
         k_top = kt[:head_dim]
 
         def body(h, carry):
@@ -131,28 +321,33 @@
 
         @pl.when(t == 0)
         def _():
-            sums[t, :head_dim, :] = dk
-            sums[t, head_dim:, :] = dv
+            for ring in rings:
+                ring[0][t, :head_dim, :] = dk[:, ring[4]]
+                ring[0][t, head_dim:, :] = dv[:, ring[4]]
 
         @pl.when(t > 0)
         def _():
-            hop(t - 1).wait_recv()
-            sums[t, :head_dim, :] += dk
-            sums[t, head_dim:, :] += dv
+            for ring in rings:
+                hop(ring, t - 1).wait_recv()
+                ring[0][t, :head_dim, :] += dk[:, ring[4]]
+                ring[0][t, head_dim:, :] += dv[:, ring[4]]
 
         @pl.when(t < nodes - 1)
         def _():
-            hop(t).start()
+            for ring in rings:
+                hop(ring, t).start()
         return c
 
     lax.fori_loop(0, nodes, step, 0)
 
     def finish(t, c):
-        hop(t).wait_send()
+        for ring in rings:
+            hop(ring, t).wait_send()
         return c
 
     lax.fori_loop(0, nodes - 1, finish, 0)
-    dkv_ref[...] = sums[nodes - 1].astype(BF16)
+    for ring in rings:
+        dkv_ref[:, ring[4]] = ring[0][nodes - 1].astype(BF16)
 
 
 def attention_backward(kt_ext, vt_ext, q_ext, do_ext, qt_ext, do_t, heads, head_dim, unroll=4):
@@ -163,7 +358,7 @@
         in_specs=[pl.BlockSpec(memory_space=pltpu.VMEM)] * 6,
         out_specs=[pl.BlockSpec(memory_space=pltpu.VMEM)] * 2,
         out_shape=[jax.ShapeDtypeStruct((2 * head_dim, bk), BF16), jax.ShapeDtypeStruct((heads * head_dim, rows), F32)],
-        scratch_shapes=[pltpu.VMEM((nodes, 2 * head_dim, bk), F32), pltpu.SemaphoreType.DMA((nodes,)), pltpu.SemaphoreType.DMA((nodes,))],
+        scratch_shapes=[pltpu.VMEM((nodes, 2 * head_dim, bk // 2), F32)] * 2 + [pltpu.SemaphoreType.DMA((nodes,))] * 4,
         compiler_params=pltpu.CompilerParams(vmem_limit_bytes=40 * 2**20, collective_id=0, has_side_effects=True),
         cost_estimate=pl.CostEstimate(flops=10 * heads * rows * nodes * bk * head_dim, bytes_accessed=2**24, transcendentals=heads * rows * nodes * bk),
         name='attention_backward',
@@ -261,22 +456,6 @@
     return dot(one_hot(recv_ix, nodes * capacity), landed.reshape(nodes * capacity, width), 0, 0).astype(BF16)
 
 
-def routes(bal_perm, bal_all, rows_dev, nodes):
-    capacity = rows_dev // nodes + rows_dev // (2 * nodes)
-    before = (lax.broadcasted_iota(jnp.int32, (rows_dev, rows_dev), 0) < lax.broadcasted_iota(jnp.int32, (rows_dev, rows_dev), 1))
-    owner = bal_perm // rows_dev
-    same = owner[:, None] == owner[None, :]
-    bal_ix = owner * capacity + jnp.sum((same & before).astype(jnp.int32), axis=0)
-    me = lax.axis_index('nodes')
-    mine = (bal_all // rows_dev == me).astype(BF16)
-    rank = dot(mine, before.astype(BF16), 1, 0).astype(jnp.int32)
-    code = lax.broadcasted_iota(jnp.int32, rank.shape, 0) * capacity + rank
-    wanted = me * rows_dev + jnp.arange(rows_dev, dtype=jnp.int32)
-    hit = bal_all.reshape(-1)[:, None] == wanted[None, :]
-    part_ix = jnp.sum(jnp.where(hit, code.reshape(-1)[:, None], 0), axis=0)
-    return bal_ix, part_ix
-
-
 def split3(x):
     keep = lambda a: lax.reduce_precision(a, 8, 7)
     hi = keep(x)
@@ -311,45 +490,35 @@
         head_dim = w_k.shape[1]
         heads = width // head_dim
         scale = head_dim ** -0.5
-        me = lax.axis_index('nodes')
-        halo_req = halo_slot.reshape(-1)
-        halo_rows = halo_req.size
+        halo_rows = halo_slot.size
 
         count = jnp.sum((valid > 0).astype(jnp.int32))
-        info = lax.all_gather(jnp.concatenate([bal_perm, halo_req, jnp.broadcast_to(count, (LANES,))]), 'nodes')
-        bal_all = info[:, :rows_dev]
-        halo_all = info[:, rows_dev:rows_dev + halo_rows].reshape(nodes, nodes, -1)
-        count_all = info[:, rows_dev + halo_rows]
-        bal_ix, part_ix = routes(bal_perm, bal_all, rows_dev, nodes)
+        info = jnp.concatenate([bal_perm, jnp.broadcast_to(count, (LANES,))])[None, None, :]
+        halo_ask = jnp.pad(halo_slot.reshape(nodes, 1, -1), ((0, 0), (0, 0), (0, LANES - halo_rows // nodes)))
+        live_dst = jnp.where(edge_mask.reshape(-1) > 0, edge_dst.reshape(-1), -1)
+        x_bal, adjacency, bal_ix, part_ix, info_all, halo_got = entry(x_feat, info, halo_ask, edge_src.reshape(-1), live_dst, nodes)
+        bal_ix, part_ix = bal_ix.reshape(-1), part_ix.reshape(-1)
+        bal_all = info_all[:, 0, :rows_dev]
         owner_all = bal_all // rows_dev
-        limit = jnp.sum(jnp.where(owner_all[:, :, None] == jnp.arange(nodes, dtype=jnp.int32), count_all[None, None, :], 0), axis=2)
-        key_bias = jnp.where(bal_all % rows_dev < limit, 0.0, NEG_FILL).astype(BF16)
-
-        x_bal = exchange(x_feat, part_ix, bal_ix, nodes)
+        limit = jnp.sum(jnp.where(owner_all[:, :, None] == jnp.arange(nodes, dtype=jnp.int32), info_all[None, None, :, 0, rows_dev], 0), axis=2)
+        key_bias = jnp.where(bal_all % rows_dev < limit, 0.0, NEG_FILL)[:, None, :]
+
         hidden_in = (x_bal.astype(F32) + pos_enc.astype(F32)).astype(BF16)
         w_kv = jnp.concatenate([w_k, w_v], axis=1)
         kv_t = dot(w_kv, hidden_in, 0, 1).astype(BF16)
-        kv_all = lax.all_gather(kv_t, 'nodes')
         wq_pad = pad_heads((w_q.astype(F32) * scale).astype(BF16), heads, 1)
         row_one = (lax.broadcasted_iota(jnp.int32, (heads * LANES, 1), 0) % LANES == head_dim).astype(F32)
         qt_ext = (dot(wq_pad, hidden_in, 0, 1) + row_one).astype(BF16)
 
-        halo_got = lax.dynamic_index_in_dim(halo_all, me, axis=1, keepdims=False).reshape(-1)
+        halo_got = halo_got[:, 0, :halo_rows // nodes].reshape(-1)
         halo_pick = one_hot(halo_got, rows_dev)
         halo_send = dot(halo_pick, x_feat, 0, 0).astype(BF16)
         halo_feat = lax.all_to_all(halo_send.reshape(nodes, -1, width), 'nodes', 0, 0, tiled=True).reshape(halo_rows, width)
-        live_dst = jnp.where(edge_mask.reshape(-1) > 0, edge_dst.reshape(-1), -1)
-        adjacency = build_adjacency(edge_src.reshape(-1), live_dst, rows_dev, rows_dev + halo_rows)
         adj_own, adj_halo = adjacency[:, :rows_dev], adjacency[:, rows_dev:]
         agg_msg = (dot(adj_own, x_feat, 1, 0) + dot(adj_halo, halo_feat, 1, 0)).astype(BF16)
         pre_act = dot(agg_msg, w_msg, 1, 0) + dot(x_feat, w_self, 1, 0)
 
-        wide = lambda n: (nodes, n, rows_dev)
-        ones3 = jnp.ones(wide(3), BF16)
-        kt_ext = jnp.concatenate([kv_all[:, :head_dim], key_bias[:, None, :], ones3, jnp.zeros(wide(LANES - head_dim - 4), BF16)], axis=1)
-        vt_ext = jnp.concatenate([kv_all[:, head_dim:], ones3, jnp.zeros(wide(LANES - head_dim - 3), BF16)], axis=1)
-        k_ext = kt_ext.transpose(0, 2, 1).reshape(nodes * rows_dev, LANES)
-        mixed_t, log_norm = attention_forward(k_ext, vt_ext, qt_ext, heads, head_dim)
+        mixed_t, log_norm, kt_ext, vt_ext = attention_forward(kv_t, key_bias, qt_ext, nodes, heads, head_dim)
         u_bal = dot(mixed_t, w_o, 0, 0).astype(BF16)
         u_part = exchange(u_bal, bal_ix, part_ix, nodes)
 

time: 512 us -> 475 us (0.928)
  waiting for transfers between devices: 84.3 us -> 53.5 us
  blocking collectives: 22.9 us -> 0 us
  Pallas kernels: 235 us -> 257 us
  other arithmetic: 12.6 us -> 7.23 us
    pallas_call x2, Pallas kernels: 84.6 us -> 111 us  [the longest x1 65.8 us: attention_forward(): pl.pallas_call(functools.partial(forward_kernel, nodes=nodes, heads=heads...]
    all_gather x1 -> x0, blocking collectives: 22.9 us -> none  [device_step(): lax.all_gather(jnp.concatenate([bal_perm, halo_req, jnp.broadcast_to(coun...]
    all_to_all x4 -> x3, waiting for transfers between devices: 60.8 us -> 43.7 us  [exchange(): lax.all_to_all(picked.reshape(nodes, capacity, width), 'nodes', 0, 0, til...]
    psum x1, waiting for transfers between devices: 23.4 us -> 9.73 us  [device_step(): lax.psum((grad_msg, grad_self, grad_o, grad_up, grad_down), 'nodes')]
    unnamed x112 -> x120, local copies, waits for them, and re-layouts: 23.5 us -> 29.6 us
    all_to_all x4 -> x3, starting transfers between devices: 25.2 us -> 21.5 us  [exchange(): lax.all_to_all(picked.reshape(nodes, capacity, width), 'nodes', 0, 0, til...]
    dot_general x37 -> x34, matrix products: 61.6 us -> 60.6 us  [dot(): lax.dot_general(a, b, (((ca,), (cb,)), ((), ())), preferred_element_type=...]
  transfers between devices with their start and end apart: 8 -> 6, of which waited for: 5 -> 4; matrix products, arithmetic and copies ran while one was open for 13% -> 11% of each run, Pallas kernels for 46% -> 46%
where the time goes in v2:
time: 475 us; the launch traced here: 465 us
  Pallas kernels  257 us (54%)
  matrix products  60.6 us (13%)
  waiting for transfers between devices  53.5 us (11%)
  local copies, waits for them, and re-layouts  38.8 us (8%)
  starting transfers between devices  32.5 us (7%)
  between operations  15 us (3%)
  other arithmetic  7.23 us (2%)
    pallas_call x1, Pallas kernels, attention_backward(): pl.pallas_call(functools.partial(backward_kernel, nodes=nodes, heads=head...  86.2 us
    pallas_call x1, Pallas kernels, attention_forward(): pl.pallas_call(functools.partial(forward_kernel, nodes=nodes, heads=heads...  65.8 us
    dot_general x34, matrix products, dot(): lax.dot_general(a, b, (((ca,), (cb,)), ((), ())), preferred_element_type=...  60.6 us
    pallas_call x1, Pallas kernels, reduce_all(): pl.pallas_call(functools.partial(reduce_kernel, nodes=nodes), in_specs=[p...  60.1 us
    pallas_call x1, Pallas kernels, entry(): pl.pallas_call(functools.partial(entry_kernel, nodes=nodes), in_specs=[pl...  45.4 us
    all_to_all x3, waiting for transfers between devices, exchange(): lax.all_to_all(picked.reshape(nodes, capacity, width), 'nodes', 0, 0, til...  43.7 us
    unnamed x120, local copies, waits for them, and re-layouts  29.6 us
    all_to_all x3, starting transfers between devices, exchange(): lax.all_to_all(picked.reshape(nodes, capacity, width), 'nodes', 0, 0, til...  21.5 us
  transfers between devices with their start and end apart: 6, of which 4 were waited for; matrix products, arithmetic and copies ran while one was open for 11% of the time, Pallas kernels for 46%

profile of v2, /device:TPU:21, one launch (start us, length us, event | category | flops | bytes accessed | tf_op | source)
XLA Modules:
  0.0 465.0 jit_solution(841565684871652317)
XLA Ops:
  7.2 1.5 convert_reduce_fusion
  8.7 1.3 concatenate.24
  11.2 1.8 reduce.13
  13.0 1.3 fusion.65
  14.4 1.0 copy-done.2
  15.4 45.4 %entry.1 = (bf16[512,512]{1,0:T(8,128)(2,1)S(1)}, bf16[512,1024]{1,0:T(8,128)(2,1)S(1)}, s32[1,512]{1,0:T(1,128)S(1)}, s32[1,512]{1,0:T(1,128)S(1)}, s32[16,1,64...) custom-call(bf16[512,512]{1,0:T(8,128)(2,1)S(1)} %copy-done.2, s32[1,1,640]{2,1,0:T(1,128)S(1)} %broadcast_in_dim.51.info_ref, ...), custom_call_target="tpu_custom_call" | custom-call | flops 26843545600 | bytes 4194304 | tf_op jit(solution)/shard_map/entry/pallas_call | solution.py:141
  61.9 1.3 convolution_convert_fusion.6
  63.2 6.4 %all-to-all-start = ((bf16[16,32,512]{2,1,0:T(8,128)(2,1)}), bf16[16,32,512]{2,1,0:T(8,128)(2,1)}, u32[]{:S(2)}, u32[]{:S(2)}) async-start(bf16[16,32,512]{2,1,0:T(8,128)(2,1)} %bitcast.106), calls=%async_computation | async-start | bytes 1048576 | tf_op jit(solution)/shard_map/all_to_all | solution.py:516
  71.6 1.2 add_convert_fusion.3
  74.6 2.1 copy.42
  76.7 2.1 pad.14
  78.8 2.0 add_convert_fusion.2.q_ref.qt_ref
  80.8 65.8 %attention_forward.1 = (bf16[512,512]{1,0:T(8,128)(2,1)S(1)}, f32[8,1,512]{2,1,0:T(1,128)S(1)}, bf16[16,128,512]{2,1,0:T(8,128)(2,1)S(1)}, bf16[16,128,512]{2,1,0:T(8,128)(2,1)S(1)}) custom-call(bf16[128,512]{1,0:T(8,128)(2,1)S(1)} %convolution_convert_fusion.7.kv_ref, f32[16,1,512]{2,1,0:T(1,128)S(1)} %compare_select_fusion.4.bias_ref, ...), custom_call_target="tpu_custom_call" | custom-call | flops 8589934592 | bytes 8388608 | tf_op jit(solution)/shard_map/attention_forward/pallas_call | solution.py:264
  146.6 1.3 copy-done.14
  147.9 1.3 copy-done.16
  149.2 1.1 pad.15
  150.4 2.9 fusion.17
  153.3 2.5 fusion.60
  155.8 7.8 %all-to-all-start.1 = ((bf16[16,48,512]{2,1,0:T(8,128)(2,1)}), bf16[16,48,512]{2,1,0:T(8,128)(2,1)}, u32[]{:S(2)}, u32[]{:S(2)}) async-start(bf16[16,48,512]{2,1,0:T(8,128)(2,1)} %bitcast.102), calls=%async_computation.1 | async-start | bytes 1572864 | tf_op jit(solution)/shard_map/all_to_all | solution.py:455
  163.6 2.0 fusion.132
  165.6 1.5 add_convert_fusion.1.q_ref
  167.3 1.5 fusion.31
  169.3 1.4 convolution_add_fusion.3
  170.8 14.3 %all-to-all-done.1 = bf16[16,48,512]{2,1,0:T(8,128)(2,1)} async-done(((bf16[16,48,512]{2,1,0:T(8,128)(2,1)}), bf16[16,48,512]{2,1,0:T(8,128)(2,1)}, u32[]{:S(2)}, u32[]{:S(2)}) %all-to-all-start.1) | async-done | bytes 786464 | tf_op jit(solution)/shard_map/all_to_all | solution.py:455
  185.0 2.1 fusion.29
  187.2 1.3 fusion.131
  189.0 3.6 fusion.2
  192.7 1.3 compare_select_fusion
  194.1 1.5 fusion.16
  196.0 1.5 fusion.134
  197.5 1.4 convolution_bitcast_fusion
  198.9 4.6 all-to-all-start.3
  203.8 1.7 convolution_convert_fusion.4
  205.5 1.4 convolution_add_fusion.1
  206.9 3.3 fusion.138
  210.2 3.8 fusion.128
  214.1 11.3 %all-to-all-done.3 = bf16[16,48,512]{2,1,0:T(8,128)(2,1)} async-done(((bf16[16,48,512]{2,1,0:T(8,128)(2,1)}), bf16[16,48,512]{2,1,0:T(8,128)(2,1)}, u32[]{:S(2)}, u32[]{:S(2)}) %all-to-all-start.3) | async-done | bytes 786464 | tf_op jit(solution)/shard_map/all_to_all | solution.py:455
  225.4 1.8 fusion.25
  227.2 1.3 bitcast_reduce_fusion
  228.4 1.4 fusion.137
  229.9 2.1 fusion.133
  232.0 1.5 add_convert_fusion.do_ref
  233.5 1.5 copy-done.15
  235.1 1.2 copy-done.7
  236.3 1.2 copy-done.8
  237.5 1.0 copy-done.11
  238.6 1.2 copy-done.13
  239.8 1.6 copy-done.17
  241.4 86.2 %attention_backward.1 = (bf16[128,512]{1,0:T(8,128)(2,1)S(1)}, f32[512,512]{1,0:T(8,128)S(1)}) custom-call(bf16[16,128,512]{2,1,0:T(8,128)(2,1)S(1)} %copy-done.15, bf16[16,128,512]{2,1,0:T(8,128)(2,1)S(1)} %copy-done.17, bf16[512,1024]{1,0:T(8,128)(2,1)S(1)} %copy-done.8, bf16[512,1024]{1,0:T(8,128)(2,1)S(1)} %copy-done.7, ...), custom_call_target="tpu_custom_call" | custom-call | flops 21474836480 | bytes 16777216 | tf_op jit(solution)/shard_map/attention_backward/pallas_call | solution.py:356
  327.7 3.2 fusion.18
  330.9 9.1 %all-to-all-start.4 = ((bf16[16,48,512]{2,1,0:T(8,128)(2,1)}), bf16[16,48,512]{2,1,0:T(8,128)(2,1)}, u32[]{:S(2)}, u32[]{:S(2)}) async-start(bf16[16,48,512]{2,1,0:T(8,128)(2,1)} %bitcast.103), calls=%async_computation.4 | async-start | bytes 1572864 | tf_op jit(solution)/shard_map/all_to_all | solution.py:455
  340.1 1.3 convolution_convert_fusion.3
  341.3 5.2 %fusion.21 = bf16[512,512]{1,0:T(8,128)(2,1)} fusion(bf16[2048,512]{1,0:T(8,128)(2,1)} %param.33, bf16[512,512]{1,0:T(8,128)(2,1)S(1)} %copy-done.42, pred[512]{0:T(512)(128)(4,1)S(1)} %get-tuple-element.70, f32[512,2048]{1,0:T(8,128)} %copy-done.29), kind=kOutput, calls=%fused_computation.42 | convolution fusion | flops 1084227584 | bytes 7340544 | tf_op jit(solution)/shard_map/dot_general | solution.py:17
  347.4 18.1 %all-to-all-done.4 = bf16[16,48,512]{2,1,0:T(8,128)(2,1)} async-done(((bf16[16,48,512]{2,1,0:T(8,128)(2,1)}), bf16[16,48,512]{2,1,0:T(8,128)(2,1)}, u32[]{:S(2)}, u32[]{:S(2)}) %all-to-all-start.4) | async-done | bytes 786464 | tf_op jit(solution)/shard_map/all_to_all | solution.py:455
  365.6 4.2 all-to-all-start.2
  369.8 60.1 %reduce_all.1 = f32[512,640]{1,0:T(8,128)S(1)} custom-call(f32[512,640]{1,0:T(8,128)S(1)} %pad_maximum_fusion.x_ref), custom_call_target="tpu_custom_call" | custom-call | flops 10000000000 | bytes 8388608 | tf_op jit(solution)/shard_map/reduce_all/pallas_call | solution.py:435
  430.0 1.1 slice.29
  432.8 1.8 fusion.26
  434.5 1.2 fusion.22
  435.8 9.7 %all-reduce.7.cloned.1.call-done = (f32[512,512]{1,0:T(8,128)}, f32[512,512]{0,1:T(8,128)}, f32[512,512]{1,0:T(8,128)}, f32[512,2048]{1,0:T(8,128)}, f32[2048,512]{1,0:T(8,128)}) async-done(((f32[512,512]{1,0:T(8,128)}, f32[512,512]{0,1:T(8,128)}, f32[512,512]{1,0:T(8,128)}, f32[512,2048]{1,0:T(8,128)}, f32[2048,512]{1,0:T(8,128)}), (f32[512,512]{1,0:T(8,128)}, f32[512,512]{0,1:T(8,128)}, ...) | async-done | bytes 11534352 | tf_op jit(solution)/shard_map/psum | solution.py:545
  445.5 2.7 copy.47
  451.2 2.1 copy.68
  453.3 1.6 copy-done.25
  454.9 2.1 copy.69
  (141 shorter events, 14.8 us)
Async XLA Ops:
  7.2 180.0 %copy-start = (bf16[512,2048]{1,0:T(8,128)(2,1)S(1)}, bf16[512,2048]{1,0:T(8,128)(2,1)}, u32[]{:S(2)}) copy-start(bf16[512,2048]{1,0:T(8,128)(2,1)} %param.32) | copy-start | bytes 6291460
  14.3 1.0 copy-start.2
  15.4 46.5 %copy-start.3 = (bf16[512,512]{1,0:T(8,128)(2,1)S(1)}, bf16[512,512]{1,0:T(8,128)(2,1)}, u32[]{:S(2)}) copy-start(bf16[512,512]{1,0:T(8,128)(2,1)} %x_ref.1) | copy-start | bytes 1572868
  60.8 1.0 copy-start.4
  61.8 8.3 %copy-start.49 = (bf16[512,64]{0,1:T(8,128)(2,1)S(1)}, bf16[512,64]{0,1:T(8,128)(2,1)}, u32[]{:S(2)}) copy-start(bf16[512,64]{0,1:T(8,128)(2,1)} %param.30) | copy-start | bytes 196612
  61.8 9.1 %copy-start.50 = (bf16[512,64]{0,1:T(8,128)(2,1)S(1)}, bf16[512,64]{0,1:T(8,128)(2,1)}, u32[]{:S(2)}) copy-start(bf16[512,64]{0,1:T(8,128)(2,1)} %param.29) | copy-start | bytes 196612
  63.2 92.6 %all-to-all-start = ((bf16[16,32,512]{2,1,0:T(8,128)(2,1)}), bf16[16,32,512]{2,1,0:T(8,128)(2,1)}, u32[]{:S(2)}, u32[]{:S(2)}) async-start(bf16[16,32,512]{2,1,0:T(8,128)(2,1)} %bitcast.106), calls=%async_computation | async-start | bytes 1048576 | tf_op jit(solution)/shard_map/all_to_all | solution.py:516
  71.6 2.1 copy-start.48
  72.8 0.9 copy-start.18
  74.6 4.2 copy-start.19
  80.7 65.8 %copy-start.12 = (bf16[1024,512]{1,0:T(8,128)(2,1)}, bf16[1024,512]{1,0:T(8,128)(2,1)S(1)}, u32[]{:S(2)}) copy-start(bf16[1024,512]{1,0:T(8,128)(2,1)S(1)} %add_convert_fusion.2.q_ref.qt_ref) | copy-start | bytes 3145732
  80.8 68.4 %copy-start.46 = (bf16[512,512]{1,0:T(8,128)(2,1)S(1)}, bf16[512,512]{1,0:T(8,128)(2,1)}, u32[]{:S(2)}) copy-start(bf16[512,512]{1,0:T(8,128)(2,1)} %param.31) | copy-start | bytes 1572868
  146.6 1.3 copy-start.14
  147.9 1.3 copy-start.16
  149.2 4.1 copy-start.9
  153.2 10.4 %copy-start.20 = (bf16[512,512]{1,0:T(8,128)(2,1)S(1)}, bf16[512,512]{1,0:T(8,128)(2,1)}, u32[]{:S(2)}) copy-start(bf16[512,512]{1,0:T(8,128)(2,1)} %copy-done.18) | copy-start | bytes 1572868
  155.8 29.3 %all-to-all-start.1 = ((bf16[16,48,512]{2,1,0:T(8,128)(2,1)}), bf16[16,48,512]{2,1,0:T(8,128)(2,1)}, u32[]{:S(2)}, u32[]{:S(2)}) async-start(bf16[16,48,512]{2,1,0:T(8,128)(2,1)} %bitcast.102), calls=%async_computation.1 | async-start | bytes 1572864 | tf_op jit(solution)/shard_map/all_to_all | solution.py:455
  165.6 1.5 copy-start.5
  165.6 1.7 copy-start.28
  167.1 1.8 copy-start.35
  167.3 2.0 copy-start.33
  168.9 1.9 copy-start.23
  187.1 1.3 copy-start.40
  187.2 1.8 copy-start.52
  187.2 1.9 copy-start.53
  188.5 4.2 copy-start.29
  189.0 3.6 copy-start.43
  192.7 1.3 copy-start.31
  194.0 3.4 copy-start.22
  194.0 1.5 copy-start.34
  194.1 1.9 copy-start.24
  197.5 6.3 %copy-start.36 = (bf16[512,512]{1,0:T(8,128)(2,1)S(1)}, bf16[512,512]{1,0:T(8,128)(2,1)}, u32[]{:S(2)}) copy-start(bf16[512,512]{1,0:T(8,128)(2,1)} %param.26) | copy-start | bytes 1572868
  198.9 6.5 %copy-start.6 = (bf16[512,1024]{1,0:T(8,128)(2,1)S(1)}, bf16[512,1024]{1,0:T(8,128)(2,1)}, u32[]{:S(2)}) copy-start(bf16[512,1024]{1,0:T(8,128)(2,1)} %copy-done.4) | copy-start | bytes 3145732
  198.9 26.5 %all-to-all-start.3 = ((bf16[16,48,512]{2,1,0:T(8,128)(2,1)}), bf16[16,48,512]{2,1,0:T(8,128)(2,1)}, u32[]{:S(2)}, u32[]{:S(2)}) async-start(bf16[16,48,512]{2,1,0:T(8,128)(2,1)} %bitcast.104), calls=%async_computation.3 | async-start | bytes 1572864 | tf_op jit(solution)/shard_map/all_to_all | solution.py:455
  203.5 242.0 %all-reduce.7.cloned.1.call-start = ((), (), s32[]{:S(2)}) async-start(), calls=%async_computation.5 | async-start | bytes 23068672 | tf_op jit(solution)/shard_map/psum | solution.py:545
  203.7 3.1 copy-start.32
  203.8 3.1 copy-start.41
  205.4 4.8 %copy-start.37 = (bf16[512,512]{1,0:T(8,128)(2,1)}, bf16[512,512]{1,0:T(8,128)(2,1)S(1)}, u32[]{:S(2)}) copy-start(bf16[512,512]{1,0:T(8,128)(2,1)S(1)} %convolution_convert_fusion.4) | copy-start | bytes 1572868
  206.9 3.3 copy-start.30
  206.9 3.3 copy-start.54
  214.1 13.1 %copy-start.10 = (bf16[512,512]{1,0:T(8,128)(2,1)S(1)}, bf16[512,512]{1,0:T(8,128)(2,1)}, u32[]{:S(2)}) copy-start(bf16[512,512]{1,0:T(8,128)(2,1)} %copy-done.9) | copy-start | bytes 1572868
  214.1 13.1 %copy-start.47 = (bf16[512,512]{1,0:T(8,128)(2,1)S(1)}, bf16[512,512]{1,0:T(8,128)(2,1)}, u32[]{:S(2)}) copy-start(bf16[512,512]{1,0:T(8,128)(2,1)} %param.31) | copy-start | bytes 1572868
  227.2 2.7 copy-start.39
  233.5 1.6 copy-start.15
  235.1 1.2 copy-start.7
  236.3 1.2 copy-start.8
  237.5 1.0 copy-start.11
  238.6 1.2 copy-start.13
  239.8 1.6 copy-start.17
  241.4 86.3 %copy-start.51 = (bf16[512,64]{1,0:T(8,128)(2,1)S(1)}, bf16[512,64]{1,0:T(8,128)(2,1)}, u32[]{:S(2)}) copy-start(bf16[512,64]{1,0:T(8,128)(2,1)} %copy.44) | copy-start | bytes 196612
  327.7 12.3 %copy-start.38 = (bf16[512,512]{1,0:T(8,128)(2,1)S(1)}, bf16[512,512]{1,0:T(8,128)(2,1)}, u32[]{:S(2)}) copy-start(bf16[512,512]{1,0:T(8,128)(2,1)} %copy-done.37) | copy-start | bytes 1572868
  330.9 10.4 %copy-start.42 = (bf16[512,512]{1,0:T(8,128)(2,1)S(1)}, bf16[512,512]{1,0:T(8,128)(2,1)}, u32[]{:S(2)}) copy-start(bf16[512,512]{1,0:T(8,128)(2,1)} %copy-done.40) | copy-start | bytes 1572868
  330.9 34.7 %all-to-all-start.4 = ((bf16[16,48,512]{2,1,0:T(8,128)(2,1)}), bf16[16,48,512]{2,1,0:T(8,128)(2,1)}, u32[]{:S(2)}, u32[]{:S(2)}) async-start(bf16[16,48,512]{2,1,0:T(8,128)(2,1)} %bitcast.103), calls=%async_computation.4 | async-start | bytes 1572864 | tf_op jit(solution)/shard_map/all_to_all | solution.py:455
  341.3 5.2 %copy-start.21 = (bf16[512,512]{1,0:T(8,128)(2,1)S(1)}, bf16[512,512]{1,0:T(8,128)(2,1)}, u32[]{:S(2)}) copy-start(bf16[512,512]{1,0:T(8,128)(2,1)} %copy-done.18) | copy-start | bytes 1572868
  365.6 68.9 %all-to-all-start.2 = ((bf16[16,32,512]{2,1,0:T(8,128)(2,1)}), bf16[16,32,512]{2,1,0:T(8,128)(2,1)S(1)}, u32[]{:S(2)}, u32[]{:S(2)}) async-start(bf16[16,32,512]{2,1,0:T(8,128)(2,1)} %bitcast.9), calls=%async_computation.2 | async-start | bytes 1048576 | tf_op jit(solution)/shard_map/all_to_all | solution.py:557
  431.1 3.5 copy-start.27
  445.5 2.7 copy-start.45
  445.5 3.7 copy-start.44
  448.2 2.9 copy-start.26
  451.1 3.7 copy-start.25
  454.9 3.1 copy-start.1
Sparse Core Ops, SparseCore 0:
  233.7 211.8 all-reduce.6
